TPU v7x, 128 devices: a whole 4x4x4 slice. The times are simulated.
128 devices in a mesh: pts: 64 (over z, x, y), grp: 2 (over core).
Axes of the slice: x: 4, y: 4, z: 4, core: 2. Of those that a mesh axis runs over, the one named last changes fastest.
Arguments:
- cam_jac: float32 [18, 1048576], P(None, ('pts', 'grp')), may hold values from -0.25 to 0.25
- pt_jac: float32 [6, 1048576], P(None, ('pts', 'grp')), may hold values from -6 to 6
- resid: float32 [2, 1048576], P(None, ('pts', 'grp')), may hold values from -102 to 102
- obs_point: int32 [1048576], P(('pts', 'grp')), may hold values from 0 to 262143, as said below
- obs_camera: int32 [1048576], P(('pts', 'grp')), may hold values from 0 to 2047
- camera_slot: int32 [2048], replicated, may hold values from 0 to 2047, each once
Outputs:
- cam_inverse: float32 [81, 2048], P(None, ('pts', 'grp'))
- precond: float32 [9, 1048576], P(None, ('pts', 'grp'))
Inputs may be any that keep to these rules, and one draw needn't show every extreme that they name: `obs_point`: observation o names a point of block o // 8192, from (o // 8192) * 2048 to (o // 8192 + 1) * 2048 - 1; within each block of 8192 observations the point number never falls and rises by at most 1 from one observation to the next, and the block's first observation names the block's first point. Each slot appears once; camera c is owned by device camera_slot[c] // 16 of the joined axes pts+grp.
All inputs are finite; a program needn't handle non-finite values.
Results may differ from a plain program's by a relative error of at most 0.0003.
Values sent between devices are 32-bit elements; how exact they have to be, the bound alone decides.
A program may use at most 64 MiB of HBM per device.

v0:
```python
import jax
import jax.numpy as jnp
from jax import lax
from jax.sharding import PartitionSpec as P

PTS_DEV = 2048


DAMP = 1.0
SPAN = 512


def split_up(value, dim, length):
    lengths = value.shape
    parts = value.reshape(*lengths[:dim], length, lengths[dim] // length, *lengths[dim + 1 :])
    return jnp.moveaxis(parts, dim, 0)


def sum_at_owner(value, axis, dim):
    length = lax.axis_size(axis)
    parts = lax.all_to_all(split_up(value, dim, length), axis, 0, 0, tiled=True)
    return jnp.sum(parts, axis=0)


def lower_pairs():
    return [(row_at, col_at) for row_at in range(9) for col_at in range(row_at + 1)]


def exact_dot(left, right):
    return jnp.dot(left, right, precision=lax.Precision.HIGHEST, preferred_element_type=jnp.float32)


def point_table(pt_jac, resid, local_point, npoints):
    entries = []
    for row_at in range(3):
        for col_at in range(row_at, 3):
            entries.append(
                pt_jac[row_at] * pt_jac[col_at] + pt_jac[3 + row_at] * pt_jac[3 + col_at]
            )
    for row_at in range(3):
        entries.append(pt_jac[row_at] * resid[0] + pt_jac[3 + row_at] * resid[1])
    stacked = jnp.stack(entries, 0)
    count = stacked.shape[1] // SPAN
    pieces = jnp.moveaxis(stacked.reshape(9, count, SPAN), 1, 0)
    point_rows = local_point.reshape(count, SPAN)
    firsts = point_rows[:, 0]
    window_ids = jnp.arange(SPAN, dtype=jnp.int32)

    def add_block(carry, inputs):
        piece, points, first = inputs
        onehot = (points[:, None] - first == window_ids[None, :]).astype(jnp.float32)
        window = lax.dynamic_slice_in_dim(carry, first, SPAN, 1)
        carry = lax.dynamic_update_slice_in_dim(carry, window + exact_dot(piece, onehot), first, 1)
        return (carry, None)

    sums, unused = lax.scan(
        add_block, jnp.zeros((9, npoints + SPAN), jnp.float32), (pieces, point_rows, firsts)
    )
    v00 = sums[0] + DAMP
    v01 = sums[1]
    v02 = sums[2]
    v11 = sums[3] + DAMP
    v12 = sums[4]
    v22 = sums[5] + DAMP
    c00 = v11 * v22 - v12 * v12
    c01 = v02 * v12 - v01 * v22
    c02 = v01 * v12 - v02 * v11
    c11 = v00 * v22 - v02 * v02
    c12 = v01 * v02 - v00 * v12
    c22 = v00 * v11 - v01 * v01
    determ = v00 * c00 + v01 * c01 + v02 * c02
    i00 = c00 / determ
    i01 = c01 / determ
    i02 = c02 / determ
    i11 = c11 / determ
    i12 = c12 / determ
    i22 = c22 / determ
    w_zero = i00 * sums[6] + i01 * sums[7] + i02 * sums[8]
    w_one = i01 * sums[6] + i11 * sums[7] + i12 * sums[8]
    w_two = i02 * sums[6] + i12 * sums[7] + i22 * sums[8]
    table = jnp.stack([i00, i01, i02, i11, i12, i22, w_zero, w_one, w_two], 0)

    def pick_block(carry, inputs):
        points, first = inputs
        onehot = (points[:, None] - first == window_ids[None, :]).astype(jnp.float32)
        window = lax.dynamic_slice_in_dim(table, first, SPAN, 1)
        return (carry, exact_dot(window, onehot.T))

    unused, picked = lax.scan(pick_block, 0, (point_rows, firsts))
    return jnp.moveaxis(picked, 0, 1).reshape(9, count * SPAN)


def obs_terms(cam_jac, pt_jac, resid, point_rows, pairs):
    i00, i01, i02, i11, i12, i22 = [point_rows[pos] for pos in range(6)]
    weights = [point_rows[6], point_rows[7], point_rows[8]]
    vinv = ((i00, i01, i02), (i01, i11, i12), (i02, i12, i22))
    prow = [[pt_jac[3 * rowp + inner] for inner in range(3)] for rowp in range(2)]
    usage = [
        [
            vinv[outer][0] * prow[rowp][0]
            + vinv[outer][1] * prow[rowp][1]
            + vinv[outer][2] * prow[rowp][2]
            for outer in range(3)
        ]
        for rowp in range(2)
    ]
    proj_zz = prow[0][0] * usage[0][0] + prow[0][1] * usage[0][1] + prow[0][2] * usage[0][2]
    proj_zo = prow[0][0] * usage[1][0] + prow[0][1] * usage[1][1] + prow[0][2] * usage[1][2]
    proj_oo = prow[1][0] * usage[1][0] + prow[1][1] * usage[1][1] + prow[1][2] * usage[1][2]
    keep = ((1.0 - proj_zz, -proj_zo), (-proj_zo, 1.0 - proj_oo))
    shifted = [
        resid[rowp]
        - (prow[rowp][0] * weights[0] + prow[rowp][1] * weights[1] + prow[rowp][2] * weights[2])
        for rowp in range(2)
    ]
    reduced = jnp.stack(
        [cam_jac[col_at] * shifted[0] + cam_jac[9 + col_at] * shifted[1] for col_at in range(9)], 0
    )
    mixed = [
        [
            keep[rowp][0] * cam_jac[col_at] + keep[rowp][1] * cam_jac[9 + col_at]
            for col_at in range(9)
        ]
        for rowp in range(2)
    ]
    terms = jnp.stack(
        [
            cam_jac[row_at] * mixed[0][col_at] + cam_jac[9 + row_at] * mixed[1][col_at]
            for row_at, col_at in pairs
        ],
        0,
    )
    return (terms, reduced)


def chol_inverse(rows, pairs):
    entry = {pair: rows[pos] for pos, pair in enumerate(pairs)}
    factor = {}
    for col_at in range(9):
        diag = entry[col_at, col_at] + DAMP
        for inner in range(col_at):
            diag = diag - factor[col_at, inner] * factor[col_at, inner]
        root = jnp.sqrt(diag)
        factor[col_at, col_at] = root
        for row_at in range(col_at + 1, 9):
            value = entry[row_at, col_at]
            for inner in range(col_at):
                value = value - factor[row_at, inner] * factor[col_at, inner]
            factor[row_at, col_at] = value / root
    solved = {}
    for col_at in range(9):
        solved[col_at, col_at] = 1.0 / factor[col_at, col_at]
        for row_at in range(col_at + 1, 9):
            value = factor[row_at, col_at] * solved[col_at, col_at]
            for inner in range(col_at + 1, row_at):
                value = value + factor[row_at, inner] * solved[inner, col_at]
            solved[row_at, col_at] = -value / factor[row_at, row_at]
    result = {}
    for row_at in range(9):
        for col_at in range(row_at + 1):
            value = solved[row_at, row_at] * solved[row_at, col_at]
            for inner in range(row_at + 1, 9):
                value = value + solved[inner, row_at] * solved[inner, col_at]
            result[row_at, col_at] = value
            result[col_at, row_at] = value
    return jnp.stack([result[row_at, col_at] for row_at in range(9) for col_at in range(9)], 0)


def apply_inverse(picked, reduced, locate):
    outputs = []
    for row_at in range(9):
        value = picked[locate[row_at, 0]] * reduced[0]
        for col_at in range(1, 9):
            value = value + picked[locate[row_at, col_at]] * reduced[col_at]
        outputs.append(value)
    return jnp.stack(outputs, 0)


def shards(cam_jac, pt_jac, resid, obs_point, obs_camera, camera_slot):
    cameras = camera_slot.shape[0]
    owned_count = cameras // lax.axis_size(("pts", "grp"))
    local_point = obs_point - lax.axis_index(("pts", "grp")) * PTS_DEV
    rows = point_table(pt_jac, resid, local_point, PTS_DEV)
    pairs = lower_pairs()
    terms, reduced = obs_terms(cam_jac, pt_jac, resid, rows, pairs)
    width = len(pairs)
    camera_of_slot = (
        jnp.zeros((cameras,), jnp.int32).at[camera_slot].set(jnp.arange(cameras, dtype=jnp.int32))
    )
    count = terms.shape[1] // SPAN
    term_blocks = jnp.moveaxis(terms.reshape(width, count, SPAN), 1, 0)
    camera_blocks = obs_camera.reshape(count, SPAN)

    def add_cameras(carry, inputs):
        piece, named = inputs
        onehot = (named[:, None] == camera_of_slot[None, :]).astype(jnp.bfloat16)
        return (carry + exact_dot(piece, onehot.astype(jnp.float32)), None)

    partial_value, unused = lax.scan(
        add_cameras, jnp.zeros((width, cameras), jnp.float32), (term_blocks, camera_blocks)
    )
    split = partial_value.reshape(width, lax.axis_size("pts"), lax.axis_size("grp"), owned_count)
    split = sum_at_owner(split, "grp", 2)
    split = sum_at_owner(split, "pts", 1)
    owned = split.reshape(width, owned_count)
    inverse = chol_inverse(owned, pairs)
    outgoing = jnp.stack([inverse[row_at * 9 + col_at] for row_at, col_at in pairs], 0)
    table = lax.all_gather(outgoing, ("pts", "grp"), axis=1, tiled=True)

    def pick_cameras(carry, named):
        onehot = (named[:, None] == camera_of_slot[None, :]).astype(jnp.bfloat16)
        return (carry, exact_dot(table, onehot.astype(jnp.float32).T))

    unused, picked = lax.scan(pick_cameras, 0, camera_blocks)
    picked = jnp.moveaxis(picked, 0, 1).reshape(width, count * SPAN)
    position = {pair: pos for pos, pair in enumerate(pairs)}
    locate = {}
    for row_at in range(9):
        for col_at in range(9):
            if (row_at, col_at) in position:
                locate[row_at, col_at] = position[row_at, col_at]
            else:
                locate[row_at, col_at] = position[col_at, row_at]
    precond = apply_inverse(picked, reduced, locate)
    return (inverse, precond)


def solution(mesh):
    in_specs = (
        P(None, ("pts", "grp")),
        P(None, ("pts", "grp")),
        P(None, ("pts", "grp")),
        P(("pts", "grp")),
        P(("pts", "grp")),
        P(),
    )
    out_specs = (P(None, ("pts", "grp")), P(None, ("pts", "grp")))
    return jax.shard_map(shards, mesh=mesh, in_specs=in_specs, out_specs=out_specs, check_vma=False)
```

profile of v0, /device:TPU:1, one launch (start us, length us, event | category | flops | bytes accessed | tf_op | source)
XLA Modules:
  0.0 349.5 jit_solution(5146475019787182314)
XLA Ops:
  1.6 1.9 multiply_add_fusion.87
  3.5 2.0 multiply_add_fusion.82
  6.0 70.6 %while.44 = (s32[]{:T(128)}, f32[9,2560]{1,0:T(8,128)S(1)}, s32[16]{0:T(128)S(1)}, f32[16,9,512]{2,1,0:T(8,128)S(1)}, s32[16,512]{1,0:T(8,128)S(1)}, /*index=5*/s32[]{:T(128)}, s32[]{:T(128)}, s32[]{:T(128)}) while((s32[]{:T(128)}, f32[9,2560]{1,0:T(8,128)S(1)}, s32[16]{0:T(128)S(1)}, f32[16,9,512]{2,1,0:T(8,128)S(1)}, ...), condition=%wide.region_1.2_spmd.clone, body=%wide.region_0.1_spmd.clone.sunk | while | flops 28578820 | bytes 127135 | solution.py:56
  77.1 64.2 %while.45 = (s32[]{:T(128)}, f32[16,9,512]{2,1,0:T(8,128)S(1)}, s32[16]{0:T(128)S(1)}, f32[9,2560]{1,0:T(8,128)S(1)}, s32[16,512]{1,0:T(8,128)S(1)}, /*index=5*/s32[]{:T(128)}, s32[]{:T(128)}, s32[]{:T(128)}) while((s32[]{:T(128)}, f32[16,9,512]{2,1,0:T(8,128)S(1)}, s32[16]{0:T(128)S(1)}, f32[9,2560]{1,0:T(8,128)S(1)}, ...), condition=%wide.region_3.4_spmd.clone, body=%wide.region_2.3_spmd.clone.sunk | while | flops 28574212 | bytes 71835 | solution.py:89
  144.5 8.2 %scatter_custom_fusion = s32[2048]{0:T(1024)S(1)} fusion(s32[2048]{0:T(1024)S(1)} %compare_select_fusion, s32[2048]{0:T(1024)S(1)} %iota.10, s32[]{:T(128)} %copy.541), kind=kCustom, calls=%fused_computation.145 | custom fusion | bytes 8196 | tf_op jit(solution)/shard_map/scatter | solution.py:188
  153.7 1.1 multiply_add_fusion.36
  158.0 6.3 %stack.335 = f32[45,16,512]{2,0,1:T(8,128)S(1)} concatenate(f32[1,16,512]{2,0,1:T(1,128)} %bitcast.291, f32[1,16,512]{2,0,1:T(1,128)} %bitcast.290, f32[1,16,512]{2,0,1:T(1,128)} %bitcast.270, f32[1,16,512]{2,0,1:T(1,128)} %bitcast.289, f32[1,16,512]{2,0,1:T(1,128)S(1)} %bitcast.269, f32[1,16,512]{2,0,1:T(1,128)} %bitcast.276, f32[1,16,512]{2,0,1:T(1,128)} %bitcast.288, ...), dimensions={0} | concatenate | bytes 2949120 | tf_op jit(solution)/shard_map/stack | solution.py:126
  164.3 38.5 %while.46 = (s32[]{:T(128)}, f32[45,2048]{1,0:T(8,128)S(1)}, f32[16,45,512]{2,1,0:T(8,128)S(1)}, s32[16,512]{1,0:T(8,128)}, s32[2048]{0:T(1024)S(1)}, /*index=5*/s32[]{:T(128)}, s32[]{:T(128)}) while((s32[]{:T(128)}, f32[45,2048]{1,0:T(8,128)S(1)}, f32[16,45,512]{2,1,0:T(8,128)S(1)}, s32[16,512]{1,0:T(8,128)}, s32[2048]{0:T(1024)S(1)}, ...), condition=%wide.region_6.7_spmd.clone, body=%wide.region_5.6_spmd.clone.sunk | while | flops 567463936 | bytes 874599 | solution.py:199
  165.0 1.7 fusion.91
  167.4 1.7 fusion.91
  169.8 1.7 fusion.91
  172.2 1.7 fusion.91
  174.6 1.7 fusion.91
  177.0 1.7 fusion.91
  179.5 1.7 fusion.91
  181.9 1.7 fusion.91
  184.3 1.7 fusion.91
  186.7 1.7 fusion.91
  189.1 1.7 fusion.91
  191.5 1.7 fusion.91
  193.9 1.7 fusion.91
  196.3 1.7 fusion.91
  198.7 1.7 fusion.91
  201.1 1.7 fusion.91
  204.5 5.0 %all_to_all.10 = f32[2,1,46080]{2,1,0:T(1,128)S(1)} all-to-all(f32[2,1,46080]{2,1,0:T(1,128)S(1)} %reshape.4789), channel_id=1, replica_groups=mesh['pts'=64,'grp'=2] {'grp'}, dimensions={0} | all-to-all | bytes 737280 | tf_op jit(solution)/shard_map/all_to_all | solution.py:21
  210.0 1.8 reduce.4
  212.7 1.2 reshape.4791
  213.9 11.5 %all-to-all-start.1 = ((f32[64,1,720]{2,1,0:T(1,128)}), f32[64,1,720]{2,1,0:T(1,128)S(1)}, u32[]{:S(2)}, u32[]{:S(2)}) async-start(f32[64,1,720]{2,1,0:T(1,128)} %reshape.4791), calls=%async_computation.1 | async-start | bytes 393216 | tf_op jit(solution)/shard_map/all_to_all | solution.py:21
  225.7 8.6 %all-to-all-done.1 = f32[64,1,720]{2,1,0:T(1,128)S(1)} async-done(((f32[64,1,720]{2,1,0:T(1,128)}), f32[64,1,720]{2,1,0:T(1,128)S(1)}, u32[]{:S(2)}, u32[]{:S(2)}) %all-to-all-start.1) | async-done | bytes 184352 | tf_op jit(solution)/shard_map/all_to_all | solution.py:21
  245.3 35.8 %all_gather.3 = f32[45,2048]{0,1:T(8,128)S(1)} all-gather(f32[45,16]{0,1:T(8,128)S(1)} %stack.337), channel_id=1, replica_groups=mesh['pts'=64,'grp'=2] {'pts','grp'}, dimensions={1}, use_global_device_ids=true | all-gather | bytes 371520 | tf_op jit(solution)/shard_map/all_gather | solution.py:208
  282.2 61.7 %while.43 = (s32[]{:T(128)}, f32[16,45,512]{2,1,0:T(8,128)S(1)}, s32[16,512]{1,0:T(8,128)}, s32[2048]{0:T(1024)S(1)}, f32[45,2048]{1,0:T(8,128)}, /*index=5*/s32[]{:T(128)}) while((s32[]{:T(128)}, f32[16,45,512]{2,1,0:T(8,128)S(1)}, s32[16,512]{1,0:T(8,128)}, s32[2048]{0:T(1024)S(1)}, f32[45,2048]{1,0:T(8,128)}, /*index=5*/s32[]{:T(128)}) %tuple.423), condition=%wide.region_10.11_spmd, body=%wide.region_9.10_spmd.sunk | while | flops 567279616 | bytes 481365 | solution.py:214
  282.9 3.1 fusion.85
  286.7 3.1 fusion.85
  290.6 3.1 fusion.85
  294.4 3.1 fusion.85
  298.3 3.1 fusion.85
  302.2 3.1 fusion.85
  306.0 3.1 fusion.85
  309.9 3.1 fusion.85
  313.7 3.1 fusion.85
  317.6 3.1 fusion.85
  321.4 3.1 fusion.85
  325.3 3.1 fusion.85
  329.2 3.1 fusion.85
  333.0 3.1 fusion.85
  336.9 3.1 fusion.85
  340.7 3.1 fusion.85
  347.7 1.8 stack.338
  (320 shorter events, 120.6 us)
Async XLA Ops:
  76.6 65.5 %copy-start = (f32[18,8192]{1,0:T(8,128)S(1)}, f32[18,8192]{1,0:T(8,128)}, u32[]{:S(2)}) copy-start(f32[18,8192]{1,0:T(8,128)} %param.14) | copy-start | bytes 1769476
  76.6 65.5 %copy-start.1 = (f32[6,8192]{1,0:T(8,128)S(1)}, f32[6,8192]{1,0:T(8,128)}, u32[]{:S(2)}) copy-start(f32[6,8192]{1,0:T(8,128)} %param.15) | copy-start | bytes 589828
  141.3 2.5 copy-start.7
  141.3 2.5 copy-start.6
  212.3 13.1 %copy-start.2 = (f32[2,8192]{1,0:T(2,128)S(1)}, f32[2,8192]{1,0:T(2,128)}, u32[]{:S(2)}) copy-start(f32[2,8192]{1,0:T(2,128)} %param.16) | copy-start | bytes 196612
  212.3 13.1 %copy-start.3 = (f32[1,16,512]{2,0,1:T(1,128)S(1)}, f32[1,16,512]{2,0,1:T(1,128)}, u32[]{:S(2)}) copy-start(f32[1,16,512]{2,0,1:T(1,128)} %get-tuple-element.485) | copy-start | bytes 98308
  212.3 13.1 %copy-start.4 = (f32[1,16,512]{2,0,1:T(1,128)S(1)}, f32[1,16,512]{2,0,1:T(1,128)}, u32[]{:S(2)}) copy-start(f32[1,16,512]{2,0,1:T(1,128)} %get-tuple-element.486) | copy-start | bytes 98308
  212.3 13.1 %copy-start.5 = (f32[1,16,512]{2,0,1:T(1,128)S(1)}, f32[1,16,512]{2,0,1:T(1,128)}, u32[]{:S(2)}) copy-start(f32[1,16,512]{2,0,1:T(1,128)} %get-tuple-element.487) | copy-start | bytes 98308
  213.9 20.4 %all-to-all-start.1 = ((f32[64,1,720]{2,1,0:T(1,128)}), f32[64,1,720]{2,1,0:T(1,128)S(1)}, u32[]{:S(2)}, u32[]{:S(2)}) async-start(f32[64,1,720]{2,1,0:T(1,128)} %reshape.4791), calls=%async_computation.1 | async-start | bytes 393216 | tf_op jit(solution)/shard_map/all_to_all | solution.py:21
where the time goes:
time: 354 us; the launch traced here: 349 us
  matrix products  93.8 us (26%)
  local copies, waits for them, and re-layouts  87.4 us (25%)
  loops' own time  66.1 us (19%)
  blocking collectives  40.8 us (12%)
  other arithmetic  40.1 us (11%)
  starting transfers between devices  11.5 us (3%)
  waiting for transfers between devices  8.62 us (2%)
    dot_general x64, matrix products, exact_dot(): jnp.dot(left, right, precision=lax.Precision.HIGHEST, preferred_element_t...  93.8 us
    dynamic_slice x64, local copies, waits for them, and re-layouts, point_table(): lax.scan(add_block, jnp.zeros((9, npoints + SPAN), jnp.float32), (pieces,...  44.2 us
    all_gather x1, blocking collectives, shards(): table = lax.all_gather(outgoing, ('pts', 'grp'), axis=1, tiled=True)  35.8 us
    another operation x1, loops' own time, point_table(): lax.scan(add_block, jnp.zeros((9, npoints + SPAN), jnp.float32), (pieces,...  32.9 us
    another operation x1, loops' own time, point_table(): unused, picked = lax.scan(pick_block, 0, (point_rows, firsts))  32.5 us
    all_to_all x1, starting transfers between devices, sum_at_owner(): parts = lax.all_to_all(split_up(value, dim, length), axis, 0, 0, tiled=True)  11.5 us
    sub x16, other arithmetic, pick_block(): points[:, None] - first == window_ids[None, :]  10.9 us
    sub x16, other arithmetic, add_block(): points[:, None] - first == window_ids[None, :]  10.9 us
  transfers between devices with their start and end apart: 1, of which 1 were waited for; matrix products, arithmetic and copies ran while one was open for 0% of the time, Pallas kernels for 0%

commit v1 on v0

v1 whole, which is shorter than its diff:
```python
import jax
import jax.numpy as jnp
from jax import lax
from jax.experimental import pallas as pl
from jax.experimental.pallas import tpu as pltpu
from jax.sharding import PartitionSpec as P

F32, BF16, I32 = jnp.float32, jnp.bfloat16, jnp.int32
MESH = pl.DeviceIdType.MESH
XS = 40
TS = 56
OS = 24
PAIRS = [(i, j) for i in range(9) for j in range(i + 1)]
CHIPS = 64


def hops(off):
    return sum(min(d, 4 - d) for d in (off // 16, off // 4 % 4, off % 4))


OFFSETS = sorted(range(1, CHIPS), key=lambda off: (-hops(off), off))


def m8(x):
    return pl.multiple_of(x, 8)


def lane_pick(row, idx):
    return jnp.take_along_axis(row, idx, axis=1, mode="promise_in_bounds")


def find_slots(cid_ref, map_ref, slot_ref):
    def step(g, carry):
        cid = cid_ref[pl.ds(m8(g * 8), 8), :]
        lo = cid & 127
        vals = [lane_pick(map_ref[pl.ds(h, 8, stride=0), :], lo) for h in range(16)]
        for b in range(4):
            bit = ((cid >> (7 + b)) & 1) == 1
            vals = [jnp.where(bit, vals[2 * i + 1], vals[2 * i]) for i in range(len(vals) // 2)]
        slot_ref[pl.ds(m8(g * 8), 8), :] = vals[0]
        return carry

    lax.fori_loop(0, 8, step, 0)


def spread_inputs(cam_ref, pt_ref, res_ref, xs):
    for j in range(64):
        at = pl.ds(j * 128, 128)
        xs[j * XS : j * XS + 8, :] = cam_ref[0:8, at]
        xs[j * XS + 8 : j * XS + 16, :] = cam_ref[8:16, at]
        xs[j * XS + 16 : j * XS + 18, :] = cam_ref[16:18, at]
        xs[j * XS + 24 : j * XS + 30, :] = pt_ref[0:6, at]
        xs[j * XS + 32 : j * XS + 34, :] = res_ref[0:2, at]


def point_sums(pid_ref, xs, tot, heads, tails, fix):
    lane = lax.broadcasted_iota(I32, (8, 128), 1)

    def quantity(g, q):
        return xs[pl.ds(g * (8 * XS) + q, 8, stride=XS), :]

    def step(g, carry):
        p = [[quantity(g, 24 + 3 * k + c) for c in range(3)] for k in range(2)]
        e = [quantity(g, 32 + k) for k in range(2)]
        pid = pid_ref[pl.ds(m8(g * 8), 8), :]
        v = [p[0][a] * p[0][c] + p[1][a] * p[1][c] for a in range(3) for c in range(a, 3)]
        v += [p[0][a] * e[0] + p[1][a] * e[1] for a in range(3)]
        end = lane
        for s in range(7):
            k = 1 << s
            same = (pltpu.roll(pid, k, 1) == pid) & (lane >= k)
            v = [x + jnp.where(same, pltpu.roll(x, k, 1), 0.0) for x in v]
            after = (pltpu.roll(pid, 128 - k, 1) == pid) & (lane < 128 - k)
            end = jnp.where(after, pltpu.roll(end, 128 - k, 1), end)
        head = jnp.zeros((8, 128), F32)
        tail = jnp.zeros((8, 128), F32)
        for q in range(9):
            full = lane_pick(v[q], end)
            tot[pl.ds(m8(q * 64 + g * 8), 8), :] = full
            head = jnp.where(lane == q, jnp.broadcast_to(full[:, 0:1], (8, 128)), head)
            tail = jnp.where(lane == q, jnp.broadcast_to(full[:, 127:128], (8, 128)), tail)
        heads[pl.ds(m8(g * 8), 8), :] = head
        tails[pl.ds(m8(g * 8), 8), :] = tail
        return carry

    lax.fori_loop(0, 8, step, 0)

    pid = pid_ref[...]
    first = jnp.broadcast_to(pid[:, 0:1], (64, 128))
    last = jnp.broadcast_to(pid[:, 127:128], (64, 128))
    ends = jnp.where(lax.broadcasted_iota(I32, (64, 128), 1) < 64, first, last).astype(F32)
    across = jnp.transpose(ends)
    r0 = lax.broadcasted_iota(I32, (64, 64), 0)
    r1 = lax.broadcasted_iota(I32, (64, 64), 1)
    from_before = (r1 < r0) & (across[64:128, :] == first[:, 0:64].astype(F32))
    from_after = (r1 > r0) & (across[0:64, :] == last[:, 0:64].astype(F32))

    def total(which, values):
        return lax.dot_general(
            jnp.where(which, 1.0, 0.0),
            values[...],
            (((1,), (0,)), ((), ())),
            precision=lax.Precision.HIGHEST,
            preferred_element_type=F32,
        )

    fix[0:64, :] = total(from_before, tails)
    fix[64:128, :] = total(from_after, heads)


def camera_sums(pid_ref, slot_ref, xs, tot, fix, red, ts, acc):
    def quantity(g, q):
        return xs[pl.ds(g * (8 * XS) + q, 8, stride=XS), :]

    def dot3(a, b):
        return a[0] * b[0] + a[1] * b[1] + a[2] * b[2]

    iota16 = lax.broadcasted_iota(I32, (16, 128), 0).astype(BF16)
    zero = jnp.zeros((16, 128), BF16)
    one = jnp.ones((16, 128), BF16)
    acc[...] = jnp.zeros((1024, 256), F32)

    def step(g, carry):
        at = pl.ds(m8(g * 8), 8)
        pid = pid_ref[at, :]
        pre = fix[at, :]
        post = fix[pl.ds(m8(64 + g * 8), 8), :]
        is_first = pid == jnp.broadcast_to(pid[:, 0:1], (8, 128))
        is_last = pid == jnp.broadcast_to(pid[:, 127:128], (8, 128))
        s = []
        for q in range(9):
            x = tot[pl.ds(m8(q * 64 + g * 8), 8), :]
            x = x + jnp.where(is_first, jnp.broadcast_to(pre[:, q : q + 1], (8, 128)), 0.0)
            x = x + jnp.where(is_last, jnp.broadcast_to(post[:, q : q + 1], (8, 128)), 0.0)
            s.append(x)
        v00, v01, v02, v11, v12, v22 = s[0] + 1.0, s[1], s[2], s[3] + 1.0, s[4], s[5] + 1.0
        c00 = v11 * v22 - v12 * v12
        c01 = v02 * v12 - v01 * v22
        c02 = v01 * v12 - v02 * v11
        c11 = v00 * v22 - v02 * v02
        c12 = v01 * v02 - v00 * v12
        c22 = v00 * v11 - v01 * v01
        inv = 1.0 / (v00 * c00 + v01 * c01 + v02 * c02)
        i00, i01, i02, i11, i12, i22 = [c * inv for c in (c00, c01, c02, c11, c12, c22)]
        vinv = ((i00, i01, i02), (i01, i11, i12), (i02, i12, i22))
        w = [dot3(vinv[a], s[6:9]) for a in range(3)]
        p = [[quantity(g, 24 + 3 * k + c) for c in range(3)] for k in range(2)]
        e = [quantity(g, 32 + k) for k in range(2)]
        use = [[dot3(vinv[a], p[k]) for a in range(3)] for k in range(2)]
        k00 = 1.0 - dot3(p[0], use[0])
        k01 = -dot3(p[0], use[1])
        k11 = 1.0 - dot3(p[1], use[1])
        sh = [e[k] - dot3(p[k], w) for k in range(2)]
        c0 = [quantity(g, c) for c in range(9)]
        c1 = [quantity(g, 9 + c) for c in range(9)]
        for c in range(9):
            red[c, at, :] = c0[c] * sh[0] + c1[c] * sh[1]
        for pos, (i, j) in enumerate(PAIRS):
            if j == 0:
                a0 = k00 * c0[i] + k01 * c1[i]
                a1 = k01 * c0[i] + k11 * c1[i]
            ts[pl.ds(g * (8 * TS) + pos, 8, stride=TS), :] = a0 * c0[j] + a1 * c1[j]
        for pos in range(45, 48):
            ts[pl.ds(g * (8 * TS) + pos, 8, stride=TS), :] = jnp.zeros((8, 128), F32)

        cols, his, units = [], [], []
        for j in range(8):
            x = ts[pl.ds(m8(g * (8 * TS) + j * TS), 48), :]
            hi = x.astype(BF16)
            lo = (x - hi.astype(F32)).astype(BF16)
            slot = jnp.broadcast_to(slot_ref[pl.ds(g * 8 + j, 1), :], (16, 128))
            odd = (slot & 1).astype(BF16)
            lo4 = ((slot >> 1) & 15).astype(BF16)
            his.append((slot >> 5).astype(BF16))
            units.append(jnp.where(lo4 == iota16, one, zero))
            parts = []
            for y in (hi, lo):
                for par in (zero, one):
                    keep = odd == par
                    parts += [jnp.where(keep, y[16 * r : 16 * r + 16, :], zero) for r in range(3)]
                    parts += [zero]
            cols.append(jnp.concatenate(parts, axis=0))
        rhs = jnp.concatenate(cols, axis=1)
        rows = []
        for v in range(64):
            mine = jnp.full((16, 128), v, BF16)
            rows.append(
                jnp.concatenate([jnp.where(his[j] == mine, units[j], zero) for j in range(8)], axis=1)
            )
        lhs = jnp.concatenate(rows, axis=0)
        acc[...] += lax.dot_general(
            lhs, rhs, (((1,), (1,)), ((), ())), preferred_element_type=F32
        )
        return carry

    lax.fori_loop(0, 8, step, 0)


def invert(owned, ent, inv_ref):
    lane = lax.broadcasted_iota(I32, (128, 128), 1)
    wide = jnp.concatenate([owned] * 16, axis=0)
    spread = lane_pick(jnp.transpose(wide), (lane & 15) >> 1)
    ent[...] = jnp.where(lane[0:64] & 1 == 0, spread[0:64], spread[64:128])
    entry = {pair: ent[pl.ds(pos, 8, stride=0), :] for pos, pair in enumerate(PAIRS)}
    factor, recip = {}, {}
    for c in range(9):
        r = lax.rsqrt(entry[c, c] + 1.0 if c == 0 else entry[c, c])
        recip[c] = r
        for i in range(c + 1, 9):
            factor[i, c] = entry[i, c] * r
        for i in range(c + 1, 9):
            for j in range(c + 1, i + 1):
                base = entry[i, j] + 1.0 if (i == j and c == 0) else entry[i, j]
                entry[i, j] = base - factor[i, c] * factor[j, c]
    solved = {}
    for c in range(9):
        solved[c, c] = recip[c]
        for i in range(c + 1, 9):
            value = factor[i, c] * solved[c, c]
            for k in range(c + 1, i):
                value = value + factor[i, k] * solved[k, c]
            solved[i, c] = -value * recip[i]
    row8 = lax.broadcasted_iota(I32, (8, 128), 0)
    lane8 = lax.broadcasted_iota(I32, (8, 128), 1)
    tile = jnp.zeros((8, 128), F32)
    for pos, (i, j) in enumerate(PAIRS):
        value = solved[i, i] * solved[i, j]
        for k in range(i + 1, 9):
            value = value + solved[k, i] * solved[k, j]
        inv_ref[9 * i + j : 9 * i + j + 1, :] = value[0:1, 0:16]
        if i != j:
            inv_ref[9 * j + i : 9 * j + i + 1, :] = value[0:1, 0:16]
        tile = jnp.where((row8 == pos // 8) & (lane8 // 16 == pos % 8), value, tile)
    return tile


def arrange(tiles, table):
    lane = lax.broadcasted_iota(I32, (8, 128), 1)

    def step(h, carry):
        x = [tiles[h * 8 + e] for e in range(8)]
        for k in (1, 2, 4):
            upper = (lane // 16) & k != 0
            for e in range(8):
                if e & k == 0:
                    low, high = x[e], x[e + k]
                    x[e] = jnp.where(upper, pltpu.roll(high, 16 * k, 1), low)
                    x[e + k] = jnp.where(upper, high, pltpu.roll(low, 128 - 16 * k, 1))
        for b in range(8):
            table[h, 8 * b : 8 * b + 8, :] = x[b]
        return carry

    lax.fori_loop(0, 16, step, 0)


def apply_inverses(table, slot_ref, red, outs, out_ref):
    def step(g, carry):
        at = pl.ds(m8(g * 8), 8)
        slot = slot_ref[at, :]
        lo = slot & 127
        bits = [((slot >> (7 + b)) & 1) == 1 for b in range(4)]
        part = [red[c, at, :] for c in range(9)]
        total = [None] * 9
        for pos, (i, j) in enumerate(PAIRS):
            row = 8 * (pos % 8) + pos // 8
            vals = [lane_pick(table[h, pl.ds(row, 8, stride=0), :], lo) for h in range(16)]
            for b in range(4):
                vals = [jnp.where(bits[b], vals[2 * n + 1], vals[2 * n]) for n in range(len(vals) // 2)]
            for r, c in sorted({(i, j), (j, i)}):
                x = vals[0] * part[c]
                total[r] = x if total[r] is None else total[r] + x
        for r in range(9):
            outs[pl.ds(g * (8 * OS) + r, 8, stride=OS), :] = total[r]
        return carry

    lax.fori_loop(0, 8, step, 0)
    for j in range(64):
        at = pl.ds(j * 128, 128)
        out_ref[0:8, at] = outs[j * OS : j * OS + 8, :]
        out_ref[8:9, at] = outs[j * OS + 8 : j * OS + 9, :]


def kernel(cam_ref, pt_ref, res_ref, pid_ref, cid_ref, map_ref, inv_ref, out_ref,
           slot_ref, xs, ts, tot, heads, tails, fix, acc, red, ent, outs, table,
           part, swap, half, recv, owned, tiles, swap_sems, send_sems, recv_sems):
    pts, core = lax.axis_index("pts"), lax.axis_index("grp")
    partner = (pts, 1 - core)

    def chip(off):
        z, x, y = pts // 16, pts // 4 % 4, pts % 4
        return ((z + off // 16) % 4) * 16 + ((x + off // 4 % 4) % 4) * 4 + (y + off % 4) % 4

    barrier = pltpu.get_barrier_semaphore()
    pl.semaphore_signal(barrier, inc=1, device_id=partner, device_id_type=MESH)
    for off in range(1, CHIPS):
        pl.semaphore_signal(barrier, inc=1, device_id=(chip(off), core), device_id_type=MESH)

    find_slots(cid_ref, map_ref, slot_ref)
    spread_inputs(cam_ref, pt_ref, res_ref, xs)
    point_sums(pid_ref, xs, tot, heads, tails, fix)
    camera_sums(pid_ref, slot_ref, xs, tot, fix, red, ts, acc)

    def fold(n, carry):
        at = pl.ds(m8(n * 16), 16)
        part[n] = (acc[at, 0:128] + acc[at, 128:256]).reshape(2, 8, 128)
        return carry

    lax.fori_loop(0, CHIPS, fold, 0)
    pl.semaphore_wait(barrier, CHIPS)

    copy = pltpu.make_async_remote_copy(
        src_ref=part.at[:, 1 - core], dst_ref=swap, send_sem=swap_sems.at[0],
        recv_sem=swap_sems.at[1], device_id=partner, device_id_type=MESH)
    copy.start()
    copy.wait()

    def join(n, carry):
        half[n] = part[n, core] + swap[n]
        return carry

    lax.fori_loop(0, CHIPS, join, 0)
    for off in OFFSETS:
        to = chip(off)
        pltpu.make_async_remote_copy(
            src_ref=half.at[to], dst_ref=recv.at[off - 1], send_sem=send_sems.at[0],
            recv_sem=recv_sems.at[0], device_id=(to, core), device_id_type=MESH).start()
    arrived = pltpu.make_async_copy(recv, recv, recv_sems.at[0])
    arrived.wait()
    pltpu.make_async_copy(recv, recv, send_sems.at[0]).wait()

    sums = [recv[n] for n in range(CHIPS - 1)] + [half[pts]]
    while len(sums) > 1:
        sums = [sums[i] + sums[i + 1] for i in range(0, len(sums) - 1, 2)] + sums[len(sums) & ~1 :]
    owned[...] = invert(sums[0], ent, inv_ref)
    tiles[pts, core] = owned[...]

    for off in OFFSETS:
        pltpu.make_async_remote_copy(
            src_ref=owned, dst_ref=tiles.at[pts, core], send_sem=send_sems.at[1],
            recv_sem=recv_sems.at[1], device_id=(chip(off), core), device_id_type=MESH).start()
    pltpu.make_async_copy(recv, recv, recv_sems.at[1]).wait()
    pltpu.make_async_copy(recv, recv, send_sems.at[1]).wait()
    copy = pltpu.make_async_remote_copy(
        src_ref=tiles.at[:, core], dst_ref=tiles.at[:, core], send_sem=swap_sems.at[2],
        recv_sem=swap_sems.at[3], device_id=partner, device_id_type=MESH)
    copy.start()
    copy.wait()
    arrange(tiles.reshape(2 * CHIPS, 8, 128), table)
    apply_inverses(table, slot_ref, red, outs, out_ref)


def shards(cam_jac, pt_jac, resid, obs_point, obs_camera, camera_slot):
    vm = pltpu.VMEM
    dma = pltpu.SemaphoreType.DMA
    return pl.pallas_call(
        kernel,
        out_shape=(jax.ShapeDtypeStruct((81, 16), F32), jax.ShapeDtypeStruct((9, 8192), F32)),
        in_specs=[pl.BlockSpec(memory_space=vm)] * 6,
        out_specs=(pl.BlockSpec(memory_space=vm), pl.BlockSpec(memory_space=vm)),
        scratch_shapes=[
            vm((64, 128), I32),
            vm((64 * XS, 128), F32),
            vm((64 * TS, 128), F32),
            vm((9 * 64, 128), F32),
            vm((64, 128), F32),
            vm((64, 128), F32),
            vm((128, 128), F32),
            vm((1024, 256), F32),
            vm((9, 64, 128), F32),
            vm((64, 128), F32),
            vm((64 * OS, 128), F32),
            vm((16, 64, 128), F32),
            vm((CHIPS, 2, 8, 128), F32),
            vm((CHIPS, 8, 128), F32),
            vm((CHIPS, 8, 128), F32),
            vm((CHIPS - 1, 8, 128), F32),
            vm((8, 128), F32),
            vm((CHIPS, 2, 8, 128), F32),
            dma((4,)),
            dma((2,)),
            dma((2,)),
        ],
        compiler_params=pltpu.CompilerParams(
            vmem_limit_bytes=58 * 2**20, collective_id=0, has_side_effects=True
        ),
        name="schur",
    )(
        cam_jac,
        pt_jac,
        resid,
        obs_point.reshape(64, 128),
        obs_camera.reshape(64, 128),
        camera_slot.reshape(16, 128),
    )


def solution(mesh):
    both = ("pts", "grp")
    in_specs = (P(None, both), P(None, both), P(None, both), P(both), P(both), P())
    out_specs = (P(None, both), P(None, both))
    return jax.shard_map(shards, mesh=mesh, in_specs=in_specs, out_specs=out_specs, check_vma=False)
```

time: 354 us -> 52.8 us (0.15); the launches traced: 349 us -> 52.5 us
  matrix products: 93.8 us -> 0 us
  local copies, waits for them, and re-layouts: 87.4 us -> 3.33 us
  loops' own time: 66.1 us -> 0 us
  Pallas kernels: 0 us -> 48.6 us
  blocking collectives: 40.8 us -> 0 us
  other arithmetic: 40.1 us -> 0 us
  starting transfers between devices: 11.5 us -> 0 us
  waiting for transfers between devices: 8.62 us -> 0 us
    dot_general x64 -> x0, matrix products: 93.8 us -> none  [exact_dot(): jnp.dot(left, right, precision=lax.Precision.HIGHEST, preferred_element_t...]
    another operation x4 -> x0, loops' own time: 66.1 us -> none  [the longest x1 32.9 us: point_table(): lax.scan(add_block, jnp.zeros((9, npoints + SPAN), jnp.float32), (pieces,...]
    pallas_call x0 -> x1, Pallas kernels: none -> 48.6 us  [shards(): pl.pallas_call(kernel, out_shape=(jax.ShapeDtypeStruct((81, 16), F32), ja...]
    dynamic_slice x64 -> x0, local copies, waits for them, and re-layouts: 44.2 us -> none  [point_table(): lax.scan(add_block, jnp.zeros((9, npoints + SPAN), jnp.float32), (pieces,...]
    all_gather x1 -> x0, blocking collectives: 35.8 us -> none  [shards(): table = lax.all_gather(outgoing, ('pts', 'grp'), axis=1, tiled=True)]
    sub x34 -> x0, other arithmetic: 22.8 us -> none  [the longest x16 10.9 us: pick_block(): points[:, None] - first == window_ids[None, :]]
    add x32 -> x0, other arithmetic: 13.8 us -> none  [the longest x9 6.9 us: obs_terms(): cam_jac[row_at] * mixed[0][col_at] + cam_jac[9 + row_at] * mixed[1][col_at]]
    all_to_all x1 -> x0, starting transfers between devices: 11.5 us -> none  [sum_at_owner(): parts = lax.all_to_all(split_up(value, dim, length), axis, 0, 0, tiled=True)]
  transfers between devices with their start and end apart: 1 -> 0, of which waited for: 1 -> 0; matrix products, arithmetic and copies ran while one was open for 0% -> 0% of each run, Pallas kernels for 0% -> 0%
where the time goes in v1:
time: 52.8 us; the launch traced here: 52.5 us
  Pallas kernels  48.6 us (92%)
  local copies, waits for them, and re-layouts  3.33 us (6%)
  between operations  0.64 us (1%)
    pallas_call x1, Pallas kernels, shards(): pl.pallas_call(kernel, out_shape=(jax.ShapeDtypeStruct((81, 16), F32), ja...  48.6 us
    unnamed x1, local copies, waits for them, and re-layouts  1.87 us
    pallas_call x1, local copies, waits for them, and re-layouts, shards(): pl.pallas_call(kernel, out_shape=(jax.ShapeDtypeStruct((81, 16), F32), ja...  1.46 us

profile of v1, /device:TPU:1, one launch (start us, length us, event | category | flops | bytes accessed | tf_op | source)
XLA Modules:
  0.0 52.5 jit_solution(11459576494455183086)
XLA Ops:
  0.6 48.6 %schur.1 = (f32[81,16]{1,0:T(8,128)}, f32[9,8192]{1,0:T(8,128)}) custom-call(f32[18,8192]{1,0:T(8,128)} %cam_ref.1, f32[6,8192]{1,0:T(8,128)} %pt_ref.1, f32[2,8192]{1,0:T(2,128)} %res_ref.1, s32[64,128]{1,0:T(8,128)} %bitcast.3, s32[64,128]{1,0:T(8,128)} %bitcast.4, s32[16,128]{1,0:T(8,128)} %bitcast.5), custom_call_target="tpu_custom_call" | custom-call | tf_op jit(solution)/shard_map/schur/pallas_call | solution.py:355
  49.2 1.5 %copy.8 = f32[81,16]{0,1:T(8,128)} copy(f32[81,16]{1,0:T(8,128)} %get-tuple-element.2) | data formatting | bytes 10368 | tf_op jit(solution)/shard_map/schur/pallas_call | solution.py:355
  50.7 1.9 %copy.10 = f32[9,8192]{1,0:T(8,128)} copy(f32[9,8192]{1,0:T(8,128)} %get-tuple-element.7) | data formatting | bytes 589824

commit v2 on v1

v2 whole, which is shorter than its diff:
```python
import jax
import jax.numpy as jnp
from jax import lax
from jax.experimental import pallas as pl
from jax.experimental.pallas import tpu as pltpu
from jax.sharding import PartitionSpec as P

F32, BF16, I32 = jnp.float32, jnp.bfloat16, jnp.int32
MESH = pl.DeviceIdType.MESH
XS = 40
TS = 56
OS = 24
PS = 40
PAIRS = [(i, j) for i in range(9) for j in range(i + 1)]
CHIPS = 64


def hops(off):
    return sum(min(d, 4 - d) for d in (off // 16, off // 4 % 4, off % 4))


OFFSETS = sorted(range(1, CHIPS), key=lambda off: (-hops(off), off))


def m8(x):
    return pl.multiple_of(x, 8)


def lane_pick(row, idx):
    return jnp.take_along_axis(row, idx, axis=1, mode="promise_in_bounds")


def find_slots(cid_ref, map_ref, slot_ref):
    for g in range(8):
        cid = cid_ref[g * 8 : g * 8 + 8, :]
        lo = cid & 127
        vals = [lane_pick(map_ref[pl.ds(h, 8, stride=0), :], lo) for h in range(16)]
        for b in range(4):
            bit = ((cid >> (7 + b)) & 1) == 1
            vals = [jnp.where(bit, vals[2 * i + 1], vals[2 * i]) for i in range(len(vals) // 2)]
        slot_ref[g * 8 : g * 8 + 8, :] = vals[0]


def spread_points(pt_ref, res_ref, xs):
    for j in range(64):
        at = pl.ds(j * 128, 128)
        xs[j * XS + 24 : j * XS + 30, :] = pt_ref[0:6, at]
        xs[j * XS + 32 : j * XS + 34, :] = res_ref[0:2, at]


def spread_cameras(cam_ref, xs):
    for j in range(64):
        at = pl.ds(j * 128, 128)
        xs[j * XS : j * XS + 8, :] = cam_ref[0:8, at]
        xs[j * XS + 8 : j * XS + 16, :] = cam_ref[8:16, at]
        xs[j * XS + 16 : j * XS + 18, :] = cam_ref[16:18, at]


def point_sums(pid_ref, xs, tot, heads, tails, fix):
    lane = lax.broadcasted_iota(I32, (8, 128), 1)

    def quantity(g, q):
        return xs[pl.ds(g * (8 * XS) + q, 8, stride=XS), :]

    def one(g):
        p = [[quantity(g, 24 + 3 * k + c) for c in range(3)] for k in range(2)]
        e = [quantity(g, 32 + k) for k in range(2)]
        pid = pid_ref[pl.ds(m8(g * 8), 8), :]
        v = [p[0][a] * p[0][c] + p[1][a] * p[1][c] for a in range(3) for c in range(a, 3)]
        v += [p[0][a] * e[0] + p[1][a] * e[1] for a in range(3)]
        return pid, v, lane

    def scan(state, k):
        pid, v, end = state
        same = (pltpu.roll(pid, k, 1) == pid) & (lane >= k)
        v = [x + jnp.where(same, pltpu.roll(x, k, 1), 0.0) for x in v]
        after = (pltpu.roll(pid, 128 - k, 1) == pid) & (lane < 128 - k)
        return pid, v, jnp.where(after, pltpu.roll(end, 128 - k, 1), end)

    def finish(g, state):
        pid, v, end = state
        head = jnp.zeros((8, 128), F32)
        tail = jnp.zeros((8, 128), F32)
        for q in range(9):
            full = lane_pick(v[q], end)
            tot[pl.ds(m8(q * 64 + g * 8), 8), :] = full
            head = jnp.where(lane == q, jnp.broadcast_to(full[:, 0:1], (8, 128)), head)
            tail = jnp.where(lane == q, jnp.broadcast_to(full[:, 127:128], (8, 128)), tail)
        heads[pl.ds(m8(g * 8), 8), :] = head
        tails[pl.ds(m8(g * 8), 8), :] = tail

    def step(n, carry):
        states = [one(n * 4 + u) for u in range(4)]
        for b in range(7):
            states = [scan(state, 1 << b) for state in states]
        for u in range(4):
            finish(n * 4 + u, states[u])
        return carry

    lax.fori_loop(0, 2, step, 0)

    pid = pid_ref[...]
    first = jnp.broadcast_to(pid[:, 0:1], (64, 128))
    last = jnp.broadcast_to(pid[:, 127:128], (64, 128))
    ends = jnp.where(lax.broadcasted_iota(I32, (64, 128), 1) < 64, first, last).astype(F32)
    across = jnp.transpose(ends)
    r0 = lax.broadcasted_iota(I32, (64, 64), 0)
    r1 = lax.broadcasted_iota(I32, (64, 64), 1)
    from_before = (r1 < r0) & (across[64:128, :] == first[:, 0:64].astype(F32))
    from_after = (r1 > r0) & (across[0:64, :] == last[:, 0:64].astype(F32))

    def total(which, values):
        return lax.dot_general(
            jnp.where(which, 1.0, 0.0),
            values[...],
            (((1,), (0,)), ((), ())),
            precision=lax.Precision.HIGHEST,
            preferred_element_type=F32,
        )

    fix[0:64, :] = total(from_before, tails)
    fix[64:128, :] = total(from_after, heads)


def camera_sums(pid_ref, slot_ref, xs, tot, fix, red, ts, rhs, acc):
    def quantity(g, q):
        return xs[pl.ds(g * (8 * XS) + q, 8, stride=XS), :]

    def dot3(a, b):
        return a[0] * b[0] + a[1] * b[1] + a[2] * b[2]

    zero = jnp.zeros((16, 128), BF16)
    one = jnp.ones((16, 128), BF16)

    def terms(g):
        at = pl.ds(g * 8, 8)
        pid = pid_ref[at, :]
        pre = fix[at, :]
        post = fix[pl.ds(64 + g * 8, 8), :]
        is_first = pid == jnp.broadcast_to(pid[:, 0:1], (8, 128))
        is_last = pid == jnp.broadcast_to(pid[:, 127:128], (8, 128))
        s = []
        for q in range(9):
            x = tot[pl.ds(q * 64 + g * 8, 8), :]
            x = x + jnp.where(is_first, jnp.broadcast_to(pre[:, q : q + 1], (8, 128)), 0.0)
            x = x + jnp.where(is_last, jnp.broadcast_to(post[:, q : q + 1], (8, 128)), 0.0)
            s.append(x)
        v00, v01, v02, v11, v12, v22 = s[0] + 1.0, s[1], s[2], s[3] + 1.0, s[4], s[5] + 1.0
        c00 = v11 * v22 - v12 * v12
        c01 = v02 * v12 - v01 * v22
        c02 = v01 * v12 - v02 * v11
        c11 = v00 * v22 - v02 * v02
        c12 = v01 * v02 - v00 * v12
        c22 = v00 * v11 - v01 * v01
        inv = 1.0 / (v00 * c00 + v01 * c01 + v02 * c02)
        i00, i01, i02, i11, i12, i22 = [c * inv for c in (c00, c01, c02, c11, c12, c22)]
        vinv = ((i00, i01, i02), (i01, i11, i12), (i02, i12, i22))
        w = [dot3(vinv[a], s[6:9]) for a in range(3)]
        p = [[quantity(g, 24 + 3 * k + c) for c in range(3)] for k in range(2)]
        e = [quantity(g, 32 + k) for k in range(2)]
        use = [[dot3(vinv[a], p[k]) for a in range(3)] for k in range(2)]
        k00 = 1.0 - dot3(p[0], use[0])
        k01 = -dot3(p[0], use[1])
        k11 = 1.0 - dot3(p[1], use[1])
        sh = [e[k] - dot3(p[k], w) for k in range(2)]
        c0 = [quantity(g, c) for c in range(9)]
        c1 = [quantity(g, 9 + c) for c in range(9)]
        for c in range(9):
            red[c, at, :] = c0[c] * sh[0] + c1[c] * sh[1]
        base = (g % 2) * (8 * TS)
        for pos, (i, j) in enumerate(PAIRS):
            if j == 0:
                a0 = k00 * c0[i] + k01 * c1[i]
                a1 = k01 * c0[i] + k11 * c1[i]
            ts[pl.ds(base + pos, 8, stride=TS), :] = a0 * c0[j] + a1 * c1[j]
        for pos in range(45, 48):
            ts[pl.ds(base + pos, 8, stride=TS), :] = jnp.zeros((8, 128), F32)

        for j in range(8):
            x = ts[base + j * TS : base + j * TS + 48, :]
            hi = x.astype(BF16)
            lo = (x - hi.astype(F32)).astype(BF16)
            slot = jnp.broadcast_to(slot_ref[g * 8 + j : g * 8 + j + 1, :], (16, 128))
            odd = (slot & 1).astype(BF16)
            parts = []
            for y in (hi, lo):
                for par in (zero, one):
                    keep = odd == par
                    parts += [jnp.where(keep, y[16 * r : 16 * r + 16, :], zero) for r in range(3)]
                    parts += [zero]
            rhs[g % 2, :, j * 128 : j * 128 + 128] = jnp.concatenate(parts, axis=0)

    def multiply(g):
        lhs = one_hot(slot_ref, g, 1, 64)
        part = lax.dot_general(
            lhs, rhs[g % 2], (((1,), (1,)), ((), ())), preferred_element_type=F32
        )
        acc[...] = part if g == 0 else acc[...] + part

    terms(0)
    for g in range(8):
        multiply(g)
        if g < 7:
            terms(g + 1)


def one_hot(slot_ref, g, shift, groups):
    iota = lax.broadcasted_iota(I32, (16, 128), 0).astype(BF16)
    zero = jnp.zeros((16, 128), BF16)
    one = jnp.ones((16, 128), BF16)
    unit, group = [], []
    for j in range(8):
        slot = jnp.broadcast_to(slot_ref[pl.ds(g * 8 + j, 1), :], (16, 128))
        unit.append(jnp.where(((slot >> shift) & 15).astype(BF16) == iota, one, zero))
        group.append(((slot >> (shift + 4)) & (groups - 1)).astype(BF16))
    rows = []
    for v in range(groups):
        mine = jnp.full((16, 128), v, BF16)
        rows.append(jnp.concatenate([jnp.where(group[j] == mine, unit[j], zero) for j in range(8)], axis=1))
    return jnp.concatenate(rows, axis=0)


def invert(owned, ent, inv_ref):
    lane = lax.broadcasted_iota(I32, (128, 128), 1)
    wide = jnp.concatenate([owned] * 16, axis=0)
    spread = lane_pick(jnp.transpose(wide), (lane & 15) >> 1)
    ent[...] = jnp.where(lane[0:64] & 1 == 0, spread[0:64], spread[64:128])
    entry = {pair: ent[pl.ds(pos, 8, stride=0), :] for pos, pair in enumerate(PAIRS)}
    factor, recip = {}, {}
    for c in range(9):
        r = lax.rsqrt(entry[c, c] + 1.0 if c == 0 else entry[c, c])
        recip[c] = r
        for i in range(c + 1, 9):
            factor[i, c] = entry[i, c] * r
        for i in range(c + 1, 9):
            for j in range(c + 1, i + 1):
                base = entry[i, j] + 1.0 if (i == j and c == 0) else entry[i, j]
                entry[i, j] = base - factor[i, c] * factor[j, c]
    solved = {}
    for c in range(9):
        solved[c, c] = recip[c]
        for i in range(c + 1, 9):
            value = factor[i, c] * solved[c, c]
            for k in range(c + 1, i):
                value = value + factor[i, k] * solved[k, c]
            solved[i, c] = -value * recip[i]
    row8 = lax.broadcasted_iota(I32, (8, 128), 0)
    lane8 = lax.broadcasted_iota(I32, (8, 128), 1)
    tile = jnp.zeros((8, 128), F32)
    for pos, (i, j) in enumerate(PAIRS):
        value = solved[i, i] * solved[i, j]
        for k in range(i + 1, 9):
            value = value + solved[k, i] * solved[k, j]
        inv_ref[9 * i + j : 9 * i + j + 1, :] = value[0:1, :]
        if i != j:
            inv_ref[9 * j + i : 9 * j + i + 1, :] = value[0:1, :]
        tile = jnp.where((row8 == pos % 8) & (lane8 // 16 == pos // 8), value, tile)
    return tile


def arrange(tiles, table, left):
    lane = lax.broadcasted_iota(I32, (8, 128), 1)
    for h in range(16):
        x = [tiles[h * 8 + e] for e in range(8)]
        for k in (1, 2, 4):
            upper = (lane // 16) & k != 0
            for e in range(8):
                if e & k == 0:
                    low, high = x[e], x[e + k]
                    x[e] = jnp.where(upper, pltpu.roll(high, 16 * k, 1), low)
                    x[e + k] = jnp.where(upper, high, pltpu.roll(low, 128 - 16 * k, 1))
        for b in (4, 5):
            table[h, 8 * (b - 4) : 8 * (b - 4) + 8, :] = x[b]
        values = jnp.concatenate(x[0:4], axis=0)
        hi = values.astype(BF16)
        lo = (values - hi.astype(F32)).astype(BF16)
        at = pl.ds(128 * (h % 4), 128)
        left[64 * (h // 4) : 64 * (h // 4) + 32, at] = hi
        left[64 * (h // 4) + 32 : 64 * (h // 4) + 64, at] = lo


def apply_inverses(table, left, slot_ref, red_ref, picked, outs, out_ref):
    for g in range(8):
        at = pl.ds(g * 8, 8)
        slot = slot_ref[at, :]
        lo = slot & 127
        bits = [((slot >> (7 + b)) & 1) == 1 for b in range(4)]
        part = [red_ref[c, at, :] for c in range(9)]
        chosen = lax.dot_general(
            left[...], one_hot(slot_ref, g, 0, 32), (((1,), (0,)), ((), ())), preferred_element_type=F32
        )
        base = (g % 2) * (8 * PS)
        for j in range(8):
            quarter = jnp.broadcast_to(slot_ref[g * 8 + j : g * 8 + j + 1, :], (8, 128)) >> 9
            low, high = (quarter & 1) == 1, quarter > 1
            for r in range(0, 32, 8):
                y = [chosen[64 * q + r : 64 * q + r + 8, 128 * j : 128 * j + 128]
                     + chosen[64 * q + 32 + r : 64 * q + 40 + r, 128 * j : 128 * j + 128] for q in range(4)]
                picked[base + PS * j + r : base + PS * j + r + 8, :] = jnp.where(
                    high, jnp.where(low, y[3], y[2]), jnp.where(low, y[1], y[0]))
        total = [None] * 9
        for pos, (i, j) in enumerate(PAIRS):
            if pos < 32:
                value = picked[pl.ds(base + pos, 8, stride=PS), :]
            else:
                vals = [lane_pick(table[h, pl.ds(pos - 32, 8, stride=0), :], lo) for h in range(16)]
                for b in range(4):
                    vals = [jnp.where(bits[b], vals[2 * n + 1], vals[2 * n]) for n in range(len(vals) // 2)]
                value = vals[0]
            for r, c in sorted({(i, j), (j, i)}):
                x = value * part[c]
                total[r] = x if total[r] is None else total[r] + x
        base = (g % 2) * (8 * OS)
        for r in range(9):
            outs[pl.ds(base + r, 8, stride=OS), :] = total[r]
        for j in range(8):
            at = pl.ds((g * 8 + j) * 128, 128)
            out_ref[0:8, at] = outs[base + j * OS : base + j * OS + 8, :]
            out_ref[8:9, at] = outs[base + j * OS + 8 : base + j * OS + 9, :]


def last(tiles, slot_ref, red_ref, rows_ref, inv_ref, out_ref, table, left, picked, outs):
    arrange(tiles, table, left)
    inv_ref[...] = jnp.transpose(rows_ref[...])[0:16, 0:81]
    apply_inverses(table, left, slot_ref, red_ref, picked, outs, out_ref)


def kernel(cam_hbm, pt_hbm, res_hbm, pid_hbm, cid_hbm, map_hbm, tiles, slot_ref, red, rows_ref,
           cam_ref, pt_ref, res_ref, pid_ref, cid_ref, map_ref,
           xs, ts, tot, heads, tails, fix, rhs, acc, ent,
           part, swap, half, recv, owned, load_sems, swap_sems, send_sems, recv_sems):
    pts, core = lax.axis_index("pts"), lax.axis_index("grp")
    partner = (pts, 1 - core)

    def chip(off):
        z, x, y = pts // 16, pts // 4 % 4, pts % 4
        return ((z + off // 16) % 4) * 16 + ((x + off // 4 % 4) % 4) * 4 + (y + off % 4) % 4

    pairs = [(cid_hbm, cid_ref), (map_hbm, map_ref), (pid_hbm, pid_ref), (pt_hbm, pt_ref),
             (res_hbm, res_ref), (cam_hbm, cam_ref)]
    loads = [pltpu.make_async_copy(src, dst, load_sems.at[n]) for n, (src, dst) in enumerate(pairs)]
    for load in loads:
        load.start()
    barrier = pltpu.get_barrier_semaphore()
    pl.semaphore_signal(barrier, inc=1, device_id=partner, device_id_type=MESH)
    for off in range(1, CHIPS):
        pl.semaphore_signal(barrier, inc=1, device_id=(chip(off), core), device_id_type=MESH)

    with jax.named_scope("load"):
        for load in loads[0:2]:
            load.wait()
    with jax.named_scope("slots"):
        find_slots(cid_ref, map_ref, slot_ref)
        for load in loads[2:5]:
            load.wait()
        spread_points(pt_ref, res_ref, xs)
    with jax.named_scope("points"):
        point_sums(pid_ref, xs, tot, heads, tails, fix)
    with jax.named_scope("cameras"):
        loads[5].wait()
        spread_cameras(cam_ref, xs)
        camera_sums(pid_ref, slot_ref, xs, tot, fix, red, ts, rhs, acc)

    with jax.named_scope("fold"):
        for n in range(CHIPS):
            at = pl.ds(n * 16, 16)
            part[n] = (acc[at, 0:128] + acc[at, 128:256]).reshape(2, 8, 128)
    with jax.named_scope("barrier"):
        pl.semaphore_wait(barrier, CHIPS)

    with jax.named_scope("swap"):
        copy = pltpu.make_async_remote_copy(
            src_ref=part.at[:, 1 - core], dst_ref=swap, send_sem=swap_sems.at[0],
            recv_sem=swap_sems.at[1], device_id=partner, device_id_type=MESH)
        copy.start()
        copy.wait()

    with jax.named_scope("scatter"):
        for n in range(CHIPS):
            half[n] = part[n, core] + swap[n]
        for off in OFFSETS:
            to = chip(off)
            pltpu.make_async_remote_copy(
                src_ref=half.at[to], dst_ref=recv.at[off - 1], send_sem=send_sems.at[0],
                recv_sem=recv_sems.at[0], device_id=(to, core), device_id_type=MESH).start()
        pltpu.make_async_copy(recv, recv, recv_sems.at[0]).wait()

    with jax.named_scope("invert"):
        sums = [recv[n] for n in range(CHIPS - 1)] + [half[pts]]
        while len(sums) > 1:
            sums = [sums[i] + sums[i + 1] for i in range(0, len(sums) - 1, 2)] + sums[len(sums) & ~1 :]
        owned[...] = invert(sums[0], ent, rows_ref)
        tiles[pts, core] = owned[...]

    with jax.named_scope("gather"):
        for off in OFFSETS:
            pltpu.make_async_remote_copy(
                src_ref=owned, dst_ref=tiles.at[pts, core], send_sem=send_sems.at[1],
                recv_sem=recv_sems.at[1], device_id=(chip(off), core), device_id_type=MESH).start()
        pltpu.make_async_copy(recv, recv, recv_sems.at[1]).wait()
    with jax.named_scope("across"):
        copy = pltpu.make_async_remote_copy(
            src_ref=tiles.at[:, core], dst_ref=tiles.at[:, core], send_sem=swap_sems.at[2],
            recv_sem=swap_sems.at[3], device_id=partner, device_id_type=MESH)
        copy.start()
        pltpu.make_async_copy(recv, recv, send_sems.at[0]).wait()
        pltpu.make_async_copy(recv, recv, send_sems.at[1]).wait()
        copy.wait()


def shards(cam_jac, pt_jac, resid, obs_point, obs_camera, camera_slot):
    vm = pltpu.VMEM
    dma = pltpu.SemaphoreType.DMA
    shape = jax.ShapeDtypeStruct
    tiles, slots, red, rows = pl.pallas_call(
        kernel,
        out_shape=(
            shape((CHIPS, 2, 8, 128), F32),
            shape((64, 128), I32),
            shape((9, 64, 128), F32),
            shape((128, 128), F32),
        ),
        in_specs=[pl.BlockSpec(memory_space=pltpu.HBM)] * 6,
        out_specs=[pl.BlockSpec(memory_space=vm)] * 4,
        scratch_shapes=[
            vm((18, 8192), F32),
            vm((6, 8192), F32),
            vm((2, 8192), F32),
            vm((64, 128), I32),
            vm((64, 128), I32),
            vm((16, 128), I32),
            vm((64 * XS, 128), F32),
            vm((16 * TS, 128), F32),
            vm((9 * 64, 128), F32),
            vm((64, 128), F32),
            vm((64, 128), F32),
            vm((128, 128), F32),
            vm((2, 256, 1024), BF16),
            vm((1024, 256), F32),
            vm((64, 128), F32),
            vm((CHIPS, 2, 8, 128), F32),
            vm((CHIPS, 8, 128), F32),
            vm((CHIPS, 8, 128), F32),
            vm((CHIPS - 1, 8, 128), F32),
            vm((8, 128), F32),
            dma((6,)),
            dma((4,)),
            dma((2,)),
            dma((2,)),
        ],
        compiler_params=pltpu.CompilerParams(
            vmem_limit_bytes=28 * 2**20, collective_id=0, has_side_effects=True
        ),
        name="schur",
    )(
        *[
            pltpu.with_memory_space_constraint(x, pltpu.HBM)
            for x in (
                cam_jac,
                pt_jac,
                resid,
                obs_point.reshape(64, 128),
                obs_camera.reshape(64, 128),
                camera_slot.reshape(16, 128),
            )
        ]
    )
    inverse, precond = pl.pallas_call(
        last,
        out_shape=(shape((16, 81), F32), shape((9, 8192), F32)),
        in_specs=[pl.BlockSpec(memory_space=vm)] * 4,
        out_specs=[pl.BlockSpec(memory_space=vm)] * 2,
        scratch_shapes=[
            vm((16, 16, 128), F32),
            vm((256, 512), BF16),
            vm((16 * PS, 128), F32),
            vm((16 * OS, 128), F32),
        ],
        compiler_params=pltpu.CompilerParams(vmem_limit_bytes=28 * 2**20),
        name="last",
    )(tiles.reshape(2 * CHIPS, 8, 128), slots, red, rows)
    return inverse.T, precond


def solution(mesh):
    both = ("pts", "grp")
    in_specs = (P(None, both), P(None, both), P(None, both), P(both), P(both), P())
    out_specs = (P(None, both), P(None, both))
    return jax.shard_map(shards, mesh=mesh, in_specs=in_specs, out_specs=out_specs, check_vma=False)
```

time: 52.8 us -> 36 us (0.68)
  Pallas kernels: 48.6 us -> 35.2 us
  local copies, waits for them, and re-layouts: 3.33 us -> 0 us
    pallas_call x1 -> x2, Pallas kernels: 48.6 us -> 35.2 us  [the longest x1 30.1 us: shards(): pl.pallas_call(kernel, out_shape=(shape((CHIPS, 2, 8, 128), F32), shape((...]
    unnamed x1 -> x0, local copies, waits for them, and re-layouts: 1.87 us -> none
    pallas_call x1 -> x0, local copies, waits for them, and re-layouts: 1.46 us -> none  [shards(): pl.pallas_call(kernel, out_shape=(jax.ShapeDtypeStruct((81, 16), F32), ja...]
where the time goes in v2:
time: 36 us; the launch traced here: 35.9 us
  Pallas kernels  35.2 us (98%)
  between operations  0.64 us (2%)
    pallas_call x1, Pallas kernels, shards(): pl.pallas_call(kernel, out_shape=(shape((CHIPS, 2, 8, 128), F32), shape((...  30.1 us
    pallas_call x1, Pallas kernels, shards(): pl.pallas_call(last, out_shape=(shape((16, 81), F32), shape((9, 8192), F3...  5.15 us

profile of v2, /device:TPU:1, one launch (start us, length us, event | category | flops | bytes accessed | tf_op | source)
XLA Modules:
  0.0 35.9 jit_solution(7556296297033530976)
XLA Ops:
  0.6 30.1 %schur.1 = (f32[64,2,8,128]{3,2,1,0:T(8,128)S(1)}, s32[64,128]{1,0:T(8,128)S(1)}, f32[9,64,128]{2,1,0:T(8,128)S(1)}, f32[128,128]{1,0:T(8,128)S(1)}) custom-call(f32[18,8192]{1,0:T(8,128)} %cam_hbm.1, f32[6,8192]{1,0:T(8,128)} %pt_hbm.1, f32[2,8192]{1,0:T(2,128)} %res_hbm.1, s32[64,128]{1,0:T(8,128)} %bitcast.6, s32[64,128]{1,0:T(8,128)} %bitcast.7, ...), custom_call_target="tpu_custom_call" | custom-call | tf_op jit(solution)/shard_map/schur/pallas_call | solution.py:415
  30.7 5.1 %last.1 = (f32[16,81]{1,0:T(8,128)}, f32[9,8192]{1,0:T(8,128)}) custom-call(f32[128,8,128]{2,1,0:T(8,128)S(1)} %bitcast.5, s32[64,128]{1,0:T(8,128)S(1)} %get-tuple-element.9.slot_ref, f32[9,64,128]{2,1,0:T(8,128)S(1)} %get-tuple-element.10.red_ref, f32[128,128]{1,0:T(8,128)S(1)} %get-tuple-element.11.rows_ref), custom_call_target="tpu_custom_call" | custom-call | tf_op jit(solution)/shard_map/last/pallas_call | solution.py:468

commit v3 on v2

v3 whole, which is shorter than its diff:
```python
import jax
import jax.numpy as jnp
import numpy as np
from jax import lax
from jax.experimental import pallas as pl
from jax.experimental.pallas import tpu as pltpu
from jax.sharding import PartitionSpec as P

F32, BF16, I32 = jnp.float32, jnp.bfloat16, jnp.int32
MESH = pl.DeviceIdType.MESH
XS = 40
TS = 56
OS = 24
PS = 56
PAIRS = [(i, j) for i in range(9) for j in range(i + 1)]
CHIPS = 64


def hops(off):
    return sum(min(d, 4 - d) for d in (off // 16, off // 4 % 4, off % 4))


OFFSETS = sorted(range(CHIPS), key=lambda off: (-hops(off), off))
RANK = {off: r for r, off in enumerate(OFFSETS)}
PARTS = 4
EACH = CHIPS // PARTS


def back(off):
    return ((-(off >> 4) & 3) << 4) | ((-(off >> 2) & 3) << 2) | (-off & 3)


def m8(x):
    return pl.multiple_of(x, 8)


def lane_pick(row, idx):
    return jnp.take_along_axis(row, idx, axis=1, mode="promise_in_bounds")


def find_slots(pts, core, cid_ref, map_ref, rank_ref, pos_ref, pick_ref):
    z, x, y = pts >> 4, (pts >> 2) & 3, pts & 3
    rank = rank_ref[...]
    for g in range(8):
        cid = cid_ref[g * 8 : g * 8 + 8, :]
        lo = cid & 127
        vals = [lane_pick(map_ref[pl.ds(h, 8, stride=0), :], lo) for h in range(16)]
        for b in range(4):
            bit = ((cid >> (7 + b)) & 1) == 1
            vals = [jnp.where(bit, vals[2 * i + 1], vals[2 * i]) for i in range(len(vals) // 2)]
        slot = vals[0]
        off = ((((slot >> 9) - z) & 3) << 4) | ((((slot >> 7) - x) & 3) << 2) | (((slot >> 5) - y) & 3)
        near = lane_pick(rank, off)
        pos_ref[g * 8 : g * 8 + 8, :] = (near << 5) | (slot & 31)
        pick_ref[g * 8 : g * 8 + 8, :] = ((((slot >> 4) & 1) ^ core) << 10) | (near << 4) | (slot & 15)


def spread_points(pt_ref, res_ref, xs):
    for j in range(64):
        at = pl.ds(j * 128, 128)
        xs[j * XS + 24 : j * XS + 30, :] = pt_ref[0:6, at]
        xs[j * XS + 32 : j * XS + 34, :] = res_ref[0:2, at]


def spread_cameras(cam_ref, xs):
    for j in range(64):
        at = pl.ds(j * 128, 128)
        xs[j * XS : j * XS + 8, :] = cam_ref[0:8, at]
        xs[j * XS + 8 : j * XS + 16, :] = cam_ref[8:16, at]
        xs[j * XS + 16 : j * XS + 18, :] = cam_ref[16:18, at]


def point_sums(pid_ref, xs, tot, heads, tails, fix, between):
    lane = lax.broadcasted_iota(I32, (8, 128), 1)

    def quantity(g, q):
        return xs[pl.ds(g * (8 * XS) + q, 8, stride=XS), :]

    def one(g):
        p = [[quantity(g, 24 + 3 * k + c) for c in range(3)] for k in range(2)]
        e = [quantity(g, 32 + k) for k in range(2)]
        pid = pid_ref[pl.ds(m8(g * 8), 8), :]
        v = [p[0][a] * p[0][c] + p[1][a] * p[1][c] for a in range(3) for c in range(a, 3)]
        v += [p[0][a] * e[0] + p[1][a] * e[1] for a in range(3)]
        return pid, v, lane

    def scan(state, k):
        pid, v, end = state
        same = (pltpu.roll(pid, k, 1) == pid) & (lane >= k)
        v = [x + jnp.where(same, pltpu.roll(x, k, 1), 0.0) for x in v]
        after = (pltpu.roll(pid, 128 - k, 1) == pid) & (lane < 128 - k)
        return pid, v, jnp.where(after, pltpu.roll(end, 128 - k, 1), end)

    def finish(g, state):
        pid, v, end = state
        head = jnp.zeros((8, 128), F32)
        tail = jnp.zeros((8, 128), F32)
        for q in range(9):
            full = lane_pick(v[q], end)
            tot[pl.ds(m8(q * 64 + g * 8), 8), :] = full
            ends = pltpu.roll(full, q + 1, 1)
            head = jnp.where(lane == q + 1, ends, head)
            tail = jnp.where(lane == q, ends, tail)
        heads[pl.ds(m8(g * 8), 8), :] = head
        tails[pl.ds(m8(g * 8), 8), :] = tail

    def step(n, carry):
        states = [one(n * 4 + u) for u in range(4)]
        for b in range(7):
            states = [scan(state, 1 << b) for state in states]
        for u in range(4):
            finish(n * 4 + u, states[u])
        return carry

    lax.fori_loop(0, 2, step, 0)
    between()

    pid = pid_ref[...]
    first = jnp.broadcast_to(pid[:, 0:1], (64, 128))
    last = jnp.broadcast_to(pid[:, 127:128], (64, 128))
    ends = jnp.where(lax.broadcasted_iota(I32, (64, 128), 1) < 64, first, last).astype(F32)
    across = jnp.transpose(ends)
    r0 = lax.broadcasted_iota(I32, (64, 64), 0)
    r1 = lax.broadcasted_iota(I32, (64, 64), 1)
    from_before = (r1 < r0) & (across[64:128, :] == first[:, 0:64].astype(F32))
    from_after = (r1 > r0) & (across[0:64, :] == last[:, 0:64].astype(F32))

    def total(which, values):
        return lax.dot_general(
            jnp.where(which, 1.0, 0.0),
            values[...],
            (((1,), (0,)), ((), ())),
            precision=lax.Precision.HIGHEST,
            preferred_element_type=F32,
        )

    fix[0:64, :] = total(from_before, tails)
    fix[64:128, :] = total(from_after, heads)


def camera_sums(pid_ref, slot_ref, xs, tot, fix, red, ts, rhs, acc, done, send):
    def quantity(g, q):
        return xs[pl.ds(g * (8 * XS) + q, 8, stride=XS), :]

    def dot3(a, b):
        return a[0] * b[0] + a[1] * b[1] + a[2] * b[2]

    def terms(g):
        at = pl.ds(g * 8, 8)
        pid = pid_ref[at, :]
        pre = fix[at, :]
        post = fix[pl.ds(64 + g * 8, 8), :]
        is_first = pid == jnp.broadcast_to(pid[:, 0:1], (8, 128))
        is_last = pid == jnp.broadcast_to(pid[:, 127:128], (8, 128))
        s = []
        for q in range(9):
            x = tot[pl.ds(q * 64 + g * 8, 8), :]
            x = x + jnp.where(is_first, jnp.broadcast_to(pre[:, q : q + 1], (8, 128)), 0.0)
            x = x + jnp.where(is_last, jnp.broadcast_to(post[:, q + 1 : q + 2], (8, 128)), 0.0)
            s.append(x)
        v00, v01, v02, v11, v12, v22 = s[0] + 1.0, s[1], s[2], s[3] + 1.0, s[4], s[5] + 1.0
        c00 = v11 * v22 - v12 * v12
        c01 = v02 * v12 - v01 * v22
        c02 = v01 * v12 - v02 * v11
        c11 = v00 * v22 - v02 * v02
        c12 = v01 * v02 - v00 * v12
        c22 = v00 * v11 - v01 * v01
        inv = 1.0 / (v00 * c00 + v01 * c01 + v02 * c02)
        i00, i01, i02, i11, i12, i22 = [c * inv for c in (c00, c01, c02, c11, c12, c22)]
        vinv = ((i00, i01, i02), (i01, i11, i12), (i02, i12, i22))
        w = [dot3(vinv[a], s[6:9]) for a in range(3)]
        p = [[quantity(g, 24 + 3 * k + c) for c in range(3)] for k in range(2)]
        e = [quantity(g, 32 + k) for k in range(2)]
        use = [[dot3(vinv[a], p[k]) for a in range(3)] for k in range(2)]
        k00 = 1.0 - dot3(p[0], use[0])
        k01 = -dot3(p[0], use[1])
        k11 = 1.0 - dot3(p[1], use[1])
        sh = [e[k] - dot3(p[k], w) for k in range(2)]
        c0 = [quantity(g, c) for c in range(9)]
        c1 = [quantity(g, 9 + c) for c in range(9)]
        for c in range(9):
            red[c, at, :] = c0[c] * sh[0] + c1[c] * sh[1]
        base = (g % 2) * (8 * TS)
        for pos, (i, j) in enumerate(PAIRS):
            if j == 0:
                a0 = k00 * c0[i] + k01 * c1[i]
                a1 = k01 * c0[i] + k11 * c1[i]
            ts[pl.ds(base + pos, 8, stride=TS), :] = a0 * c0[j] + a1 * c1[j]
        for pos in range(45, 48):
            ts[pl.ds(base + pos, 8, stride=TS), :] = jnp.zeros((8, 128), F32)

        for j in range(8):
            x = ts[base + j * TS : base + j * TS + 48, :]
            odd = jnp.broadcast_to(slot_ref[g * 8 + j : g * 8 + j + 1, :] & 1, (48, 128)) == 1
            none = jnp.zeros((16, 128), F32)
            both = [jnp.where(odd, 0.0, x), none, jnp.where(odd, x, 0.0), none]
            x = jnp.transpose(jnp.concatenate(both, axis=0))
            hi = x.astype(BF16)
            rhs[g, j * 128 : j * 128 + 128, 0:128] = hi
            rhs[g, j * 128 : j * 128 + 128, 128:256] = (x - hi.astype(F32)).astype(BF16)

    def multiply(n, g):
        for k in (2 * n, 2 * n + 1):
            count = 32 // PARTS
            lhs = one_hot(slot_ref, g, 1, k * count, count)
            part = lax.dot_general(lhs, rhs[g], (((1,), (0,)), ((), ())), preferred_element_type=F32)
            at = pl.ds(k * 16 * count, 16 * count)
            acc[at, :] = part if g == 0 else acc[at, :] + part

    terms(0)
    for n in range(PARTS):
        for g in range(8):
            multiply(n, g)
            if n == 0 and g < 7:
                terms(g + 1)
            if g == 6 and n > 0:
                send(n - 1)
        done(n)


def one_hot(slot_ref, g, shift, start, groups, mask=63, upper=None):
    iota = lax.broadcasted_iota(I32, (16, 128), 0).astype(BF16)
    zero = jnp.zeros((16, 128), BF16)
    one = jnp.ones((16, 128), BF16)
    unit, group = [], []
    for j in range(8):
        slot = jnp.broadcast_to(slot_ref[pl.ds(g * 8 + j, 1), :], (16, 128))
        low = (slot >> shift) & 15
        if upper is not None:
            low = jnp.where((slot >> 10) == upper, low, 16)
        unit.append(jnp.where(low.astype(BF16) == iota, one, zero))
        group.append(((slot >> (shift + 4)) & mask).astype(BF16))
    rows = []
    for v in range(start, start + groups):
        mine = jnp.full((16, 128), v, BF16)
        rows.append(jnp.concatenate([jnp.where(group[j] == mine, unit[j], zero) for j in range(8)], axis=1))
    return jnp.concatenate(rows, axis=0)


def invert(owned, ent, inv_ref):
    lane = lax.broadcasted_iota(I32, (128, 128), 1)
    wide = jnp.concatenate([owned] * 16, axis=0)
    spread = lane_pick(jnp.transpose(wide), (lane & 15) >> 1)
    ent[...] = jnp.where(lane[0:64] & 1 == 0, spread[0:64], spread[64:128])
    entry = {pair: ent[pl.ds(pos, 8, stride=0), :] for pos, pair in enumerate(PAIRS)}
    factor, recip = {}, {}
    for c in range(9):
        r = lax.rsqrt(entry[c, c] + 1.0 if c == 0 else entry[c, c])
        recip[c] = r
        for i in range(c + 1, 9):
            factor[i, c] = entry[i, c] * r
        for i in range(c + 1, 9):
            for j in range(c + 1, i + 1):
                base = entry[i, j] + 1.0 if (i == j and c == 0) else entry[i, j]
                entry[i, j] = base - factor[i, c] * factor[j, c]
    solved = {}
    for c in range(9):
        solved[c, c] = recip[c]
        for i in range(c + 1, 9):
            value = factor[i, c] * solved[c, c]
            for k in range(c + 1, i):
                value = value + factor[i, k] * solved[k, c]
            solved[i, c] = -value * recip[i]
    row8 = lax.broadcasted_iota(I32, (8, 128), 0)
    lane8 = lax.broadcasted_iota(I32, (8, 128), 1)
    tile = jnp.zeros((8, 128), F32)
    for pos, (i, j) in enumerate(PAIRS):
        value = solved[i, i] * solved[i, j]
        for k in range(i + 1, 9):
            value = value + solved[k, i] * solved[k, j]
        inv_ref[9 * i + j : 9 * i + j + 1, :] = value[0:1, :]
        if i != j:
            inv_ref[9 * j + i : 9 * j + i + 1, :] = value[0:1, :]
        tile = jnp.where((row8 == pos % 8) & (lane8 // 16 == pos // 8), value, tile)
    return tile


def arrange(tiles, left):
    lane = lax.broadcasted_iota(I32, (8, 128), 1)
    for h in range(8):
        x = [tiles[h * 8 + e] for e in range(8)]
        for k in (1, 2, 4):
            upper = (lane // 16) & k != 0
            for e in range(8):
                if e & k == 0:
                    low, high = x[e], x[e + k]
                    x[e] = jnp.where(upper, pltpu.roll(high, 16 * k, 1), low)
                    x[e + k] = jnp.where(upper, high, pltpu.roll(low, 128 - 16 * k, 1))
        values = jnp.concatenate(x[0:6], axis=0)
        hi = values.astype(BF16)
        lo = (values - hi.astype(F32)).astype(BF16)
        at = pl.ds(128 * (h % 2), 128)
        left[96 * (h // 2) : 96 * (h // 2) + 48, at] = hi
        left[96 * (h // 2) + 48 : 96 * (h // 2) + 96, at] = lo


def choose(left, pick_ref, g, upper, store):
    chosen = lax.dot_general(
        left[...], one_hot(pick_ref, g, 0, 0, 16, 15, upper), (((1,), (0,)), ((), ())),
        preferred_element_type=F32,
    )
    for j in range(8):
        quarter = (jnp.broadcast_to(pick_ref[g * 8 + j : g * 8 + j + 1, :], (8, 128)) >> 8) & 3
        low, high = (quarter & 1) == 1, quarter > 1
        at = slice(128 * j, 128 * j + 128)
        for r in range(0, 48, 8):
            y = [chosen[96 * q + r : 96 * q + r + 8, at] + chosen[96 * q + 48 + r : 96 * q + 56 + r, at]
                 for q in range(4)]
            store(j, r, jnp.where(high, jnp.where(low, y[3], y[2]), jnp.where(low, y[1], y[0])))


def last(theirs, pick_ref, red_ref, rows_ref, near_ref, inv_ref, out_ref, left, picked, outs):
    arrange(theirs, left)
    inv_ref[...] = jnp.transpose(rows_ref[...])[0:16, 0:81]
    for g in range(8):
        base = (g % 2) * (8 * PS)

        def store(j, r, value):
            at = (g * 8 + j) * 48 + r
            picked[base + PS * j + r : base + PS * j + r + 8, :] = value + near_ref[at : at + 8, :]

        choose(left, pick_ref, g, 1, store)
        part = [red_ref[c, g * 8 : g * 8 + 8, :] for c in range(9)]
        total = [None] * 9
        for pos, (i, j) in enumerate(PAIRS):
            value = picked[pl.ds(base + pos, 8, stride=PS), :]
            for r, c in sorted({(i, j), (j, i)}):
                x = value * part[c]
                total[r] = x if total[r] is None else total[r] + x
        base = (g % 2) * (8 * OS)
        for r in range(9):
            outs[pl.ds(base + r, 8, stride=OS), :] = total[r]
        for j in range(8):
            at = pl.ds((g * 8 + j) * 128, 128)
            out_ref[0:8, at] = outs[base + j * OS : base + j * OS + 8, :]
            out_ref[8:9, at] = outs[base + j * OS + 8 : base + j * OS + 9, :]


def kernel(cam_hbm, pt_hbm, res_hbm, pid_hbm, cid_hbm, map_hbm, rank_hbm, theirs, pick_ref, red, rows_ref, near_ref,
           cam_ref, pt_ref, res_ref, pid_ref, cid_ref, map_ref, rank_ref, pos_ref,
           xs, ts, tot, heads, tails, fix, rhs, acc, ent,
           part, swap, half, recv, owned, mine, left, load_sems, swap_sems, send_sems, recv_sems):
    pts, core = lax.axis_index("pts"), lax.axis_index("grp")
    partner = (pts, 1 - core)
    chip_z = [(((pts >> 4) + d) & 3) << 4 for d in range(4)]
    chip_x = [(((pts >> 2) + d) & 3) << 2 for d in range(4)]
    chip_y = [(pts + d) & 3 for d in range(4)]

    def chip(off):
        return chip_z[off >> 4] + chip_x[(off >> 2) & 3] + chip_y[off & 3]

    pairs = [(cid_hbm, cid_ref), (map_hbm, map_ref), (rank_hbm, rank_ref), (pid_hbm, pid_ref),
             (pt_hbm, pt_ref), (res_hbm, res_ref), (cam_hbm, cam_ref)]
    loads = [pltpu.make_async_copy(src, dst, load_sems.at[n]) for n, (src, dst) in enumerate(pairs)]
    for load in loads:
        load.start()
    barrier = pltpu.get_barrier_semaphore()
    peers = [partner] + [(chip(off), core) for off in OFFSETS[:-1]]
    for peer in peers:
        pl.semaphore_signal(barrier, inc=1, device_id=peer, device_id_type=MESH)

    with jax.named_scope("load"):
        for load in loads[0:3]:
            load.wait()
    with jax.named_scope("slots"):
        find_slots(pts, core, cid_ref, map_ref, rank_ref, pos_ref, pick_ref)
        for load in loads[3:6]:
            load.wait()
        spread_points(pt_ref, res_ref, xs)

    def cameras_in():
        loads[6].wait()
        spread_cameras(cam_ref, xs)

    def swap_of(n):
        some = pl.ds(n * EACH, EACH)
        return pltpu.make_async_remote_copy(
            src_ref=part.at[some, 1 - core], dst_ref=swap.at[some], send_sem=swap_sems.at[n],
            recv_sem=swap_sems.at[PARTS + n], device_id=partner, device_id_type=MESH)

    def send(n):
        swap_of(n).wait()
        for r in range(n * EACH, n * EACH + EACH):
            half[r] = part[r, core] + swap[r]
        for r in range(n * EACH, n * EACH + EACH):
            if OFFSETS[r]:
                pltpu.make_async_remote_copy(
                    src_ref=half.at[r], dst_ref=recv.at[r], send_sem=send_sems.at[0],
                    recv_sem=recv_sems.at[0], device_id=(chip(OFFSETS[r]), core), device_id_type=MESH).start()

    def done(n):
        with jax.named_scope("send"):
            for r in range(n * EACH, n * EACH + EACH):
                at = pl.ds(r * 16, 16)
                part[r] = (acc[at, 0:128] + acc[at, 128:256]).reshape(2, 8, 128)
            if n == 0:
                pl.semaphore_wait(barrier, len(peers))
            swap_of(n).start()

    with jax.named_scope("points"):
        point_sums(pid_ref, xs, tot, heads, tails, fix, cameras_in)
    with jax.named_scope("cameras"):
        camera_sums(pid_ref, pos_ref, xs, tot, fix, red, ts, rhs, acc, done, send)
    with jax.named_scope("scatter"):
        send(PARTS - 1)
        pltpu.make_async_copy(recv, recv, recv_sems.at[0]).wait()

    with jax.named_scope("invert"):
        sums = [recv[n] for n in range(CHIPS - 1)] + [half[CHIPS - 1]]
        while len(sums) > 1:
            sums = [sums[i] + sums[i + 1] for i in range(0, len(sums), 2)]
        owned[...] = invert(sums[0], ent, rows_ref)
        mine[CHIPS - 1] = owned[...]

    with jax.named_scope("gather"):
        for off in OFFSETS[:-1]:
            pltpu.make_async_remote_copy(
                src_ref=owned, dst_ref=mine.at[RANK[back(off)]], send_sem=send_sems.at[1],
                recv_sem=recv_sems.at[1], device_id=(chip(off), core), device_id_type=MESH).start()
        pltpu.make_async_copy(recv, recv, recv_sems.at[1]).wait()
    with jax.named_scope("near"):
        across = pltpu.make_async_remote_copy(
            src_ref=mine, dst_ref=theirs, send_sem=swap_sems.at[0], recv_sem=swap_sems.at[PARTS],
            device_id=partner, device_id_type=MESH)
        across.start()
        arrange(mine, left)
        for g in range(8):
            def store(j, r, value):
                at = (g * 8 + j) * 48 + r
                near_ref[at : at + 8, :] = value

            choose(left, pick_ref, g, 0, store)
    with jax.named_scope("across"):
        pltpu.make_async_copy(recv, recv, send_sems.at[0]).wait()
        pltpu.make_async_copy(recv, recv, send_sems.at[1]).wait()
        across.wait()


def shards(cam_jac, pt_jac, resid, obs_point, obs_camera, camera_slot):
    vm = pltpu.VMEM
    dma = pltpu.SemaphoreType.DMA
    shape = jax.ShapeDtypeStruct
    ranks = np.zeros((8, 128), np.int32)
    ranks[:, OFFSETS] = np.arange(CHIPS)
    ranks = jnp.asarray(ranks)
    theirs, picks, red, rows, near = pl.pallas_call(
        kernel,
        out_shape=(
            shape((CHIPS, 8, 128), F32),
            shape((64, 128), I32),
            shape((9, 64, 128), F32),
            shape((128, 128), F32),
            shape((64 * 48, 128), F32),
        ),
        in_specs=[pl.BlockSpec(memory_space=pltpu.HBM)] * 7,
        out_specs=[pl.BlockSpec(memory_space=vm)] * 5,
        scratch_shapes=[
            vm((18, 8192), F32),
            vm((6, 8192), F32),
            vm((2, 8192), F32),
            vm((64, 128), I32),
            vm((64, 128), I32),
            vm((16, 128), I32),
            vm((8, 128), I32),
            vm((64, 128), I32),
            vm((64 * XS, 128), F32),
            vm((16 * TS, 128), F32),
            vm((9 * 64, 128), F32),
            vm((64, 128), F32),
            vm((64, 128), F32),
            vm((128, 128), F32),
            vm((8, 1024, 256), BF16),
            vm((1024, 256), F32),
            vm((64, 128), F32),
            vm((CHIPS, 2, 8, 128), F32),
            vm((CHIPS, 8, 128), F32),
            vm((CHIPS, 8, 128), F32),
            vm((CHIPS - 1, 8, 128), F32),
            vm((8, 128), F32),
            vm((CHIPS, 8, 128), F32),
            vm((384, 256), BF16),
            dma((7,)),
            dma((2 * PARTS,)),
            dma((2,)),
            dma((6,)),
        ],
        compiler_params=pltpu.CompilerParams(
            vmem_limit_bytes=28 * 2**20, collective_id=0, has_side_effects=True
        ),
        name="schur",
    )(
        *[
            pltpu.with_memory_space_constraint(x, pltpu.HBM)
            for x in (
                cam_jac,
                pt_jac,
                resid,
                obs_point.reshape(64, 128),
                obs_camera.reshape(64, 128),
                camera_slot.reshape(16, 128),
                ranks,
            )
        ]
    )
    inverse, precond = pl.pallas_call(
        last,
        out_shape=(shape((16, 81), F32), shape((9, 8192), F32)),
        in_specs=[pl.BlockSpec(memory_space=vm)] * 5,
        out_specs=[pl.BlockSpec(memory_space=vm)] * 2,
        scratch_shapes=[
            vm((384, 256), BF16),
            vm((16 * PS, 128), F32),
            vm((16 * OS, 128), F32),
        ],
        compiler_params=pltpu.CompilerParams(vmem_limit_bytes=28 * 2**20),
        name="last",
    )(theirs, picks, red, rows, near)
    return inverse.T, precond


def solution(mesh):
    both = ("pts", "grp")
    in_specs = (P(None, both), P(None, both), P(None, both), P(both), P(both), P())
    out_specs = (P(None, both), P(None, both))
    return jax.shard_map(shards, mesh=mesh, in_specs=in_specs, out_specs=out_specs, check_vma=False)
```

time: 36 us -> 32.6 us (0.906)
  Pallas kernels: 35.2 us -> 31.8 us
    pallas_call x1, Pallas kernels: 5.15 us -> 3.07 us  [shards(): pl.pallas_call(last, out_shape=(shape((16, 81), F32), shape((9, 8192), F3...]
    pallas_call x1, Pallas kernels: 30.1 us -> 28.8 us  [shards(): pl.pallas_call(kernel, out_shape=(shape((CHIPS, 8, 128), F32), shape((64,...]
where the time goes in v3:
time: 32.6 us; the launch traced here: 32.5 us
  Pallas kernels  31.8 us (98%)
  between operations  0.64 us (2%)
    pallas_call x1, Pallas kernels, shards(): pl.pallas_call(kernel, out_shape=(shape((CHIPS, 8, 128), F32), shape((64,...  28.8 us
    pallas_call x1, Pallas kernels, shards(): pl.pallas_call(last, out_shape=(shape((16, 81), F32), shape((9, 8192), F3...  3.07 us

profile of v3, /device:TPU:1, one launch (start us, length us, event | category | flops | bytes accessed | tf_op | source)
XLA Modules:
  0.0 32.5 jit_solution(7680245818484645817)
XLA Ops:
  0.6 28.8 %schur.1 = (f32[64,8,128]{2,1,0:T(8,128)S(1)}, s32[64,128]{1,0:T(8,128)S(1)}, f32[9,64,128]{2,1,0:T(8,128)S(1)}, f32[128,128]{1,0:T(8,128)S(1)}, f32[3072,128]{1,0:T(8,128)S(1)}) custom-call(f32[18,8192]{1,0:T(8,128)} %cam_hbm.1, f32[6,8192]{1,0:T(8,128)} %pt_hbm.1, f32[2,8192]{1,0:T(2,128)} %res_hbm.1, s32[64,128]{1,0:T(8,128)} %bitcast.4, ...), custom_call_target="tpu_custom_call" | custom-call | tf_op jit(solution)/shard_map/schur/pallas_call | solution.py:446
  29.4 3.1 %last.1 = (f32[16,81]{1,0:T(8,128)}, f32[9,8192]{1,0:T(8,128)}) custom-call(f32[64,8,128]{2,1,0:T(8,128)S(1)} %get-tuple-element.9.theirs, s32[64,128]{1,0:T(8,128)S(1)} %get-tuple-element.10.pick_ref, f32[9,64,128]{2,1,0:T(8,128)S(1)} %get-tuple-element.11.red_ref, f32[128,128]{1,0:T(8,128)S(1)} %get-tuple-element.12.rows_ref, ...), custom_call_target="tpu_custom_call" | custom-call | tf_op jit(solution)/shard_map/last/pallas_call | solution.py:505

commit v4 on v3

--- a/solution.py
+++ b/solution.py
@@ -24,6 +24,8 @@
 RANK = {off: r for r, off in enumerate(OFFSETS)}
 PARTS = 4
 EACH = CHIPS // PARTS
+AHEAD = 5
+CLOSE = 3 * EACH
 
 
 def back(off):
@@ -208,14 +210,28 @@
             acc[at, :] = part if g == 0 else acc[at, :] + part
 
     terms(0)
-    for n in range(PARTS):
-        for g in range(8):
-            multiply(n, g)
-            if n == 0 and g < 7:
-                terms(g + 1)
-            if g == 6 and n > 0:
-                send(n - 1)
-        done(n)
+    for g in range(8):
+        multiply(0, g)
+        if g < AHEAD:
+            multiply(1, g)
+        if g < 7:
+            terms(g + 1)
+    done(0)
+    for g in range(AHEAD, 8):
+        multiply(1, g)
+    done(1)
+    for g in range(8):
+        multiply(2, g)
+        if g == 3:
+            send(0)
+    done(2)
+    for g in range(8):
+        multiply(3, g)
+        if g == 0:
+            send(1)
+        if g == 6:
+            send(2)
+    done(3)
 
 
 def one_hot(slot_ref, g, shift, start, groups, mask=63, upper=None):
@@ -349,27 +365,26 @@
     def chip(off):
         return chip_z[off >> 4] + chip_x[(off >> 2) & 3] + chip_y[off & 3]
 
-    pairs = [(cid_hbm, cid_ref), (map_hbm, map_ref), (rank_hbm, rank_ref), (pid_hbm, pid_ref),
-             (pt_hbm, pt_ref), (res_hbm, res_ref), (cam_hbm, cam_ref)]
+    pairs = [(pt_hbm, pt_ref), (res_hbm, res_ref), (pid_hbm, pid_ref), (cid_hbm, cid_ref),
+             (map_hbm, map_ref), (rank_hbm, rank_ref), (cam_hbm, cam_ref)]
     loads = [pltpu.make_async_copy(src, dst, load_sems.at[n]) for n, (src, dst) in enumerate(pairs)]
     for load in loads:
         load.start()
     barrier = pltpu.get_barrier_semaphore()
     peers = [partner] + [(chip(off), core) for off in OFFSETS[:-1]]
+    peers += [(chip(off), 1 - core) for off in OFFSETS[:-1] if off in OFFSETS[CLOSE:] or back(off) in OFFSETS[CLOSE:]]
     for peer in peers:
         pl.semaphore_signal(barrier, inc=1, device_id=peer, device_id_type=MESH)
 
     with jax.named_scope("load"):
         for load in loads[0:3]:
             load.wait()
-    with jax.named_scope("slots"):
+        spread_points(pt_ref, res_ref, xs)
+
+    def cameras_in():
+        for load in loads[3:]:
+            load.wait()
         find_slots(pts, core, cid_ref, map_ref, rank_ref, pos_ref, pick_ref)
-        for load in loads[3:6]:
-            load.wait()
-        spread_points(pt_ref, res_ref, xs)
-
-    def cameras_in():
-        loads[6].wait()
         spread_cameras(cam_ref, xs)
 
     def swap_of(n):
@@ -378,15 +393,17 @@
             src_ref=part.at[some, 1 - core], dst_ref=swap.at[some], send_sem=swap_sems.at[n],
             recv_sem=swap_sems.at[PARTS + n], device_id=partner, device_id_type=MESH)
 
+    def give(src, slot, device):
+        pltpu.make_async_remote_copy(
+            src_ref=src, dst_ref=recv.at[slot], send_sem=send_sems.at[0], recv_sem=recv_sems.at[0],
+            device_id=device, device_id_type=MESH).start()
+
     def send(n):
         swap_of(n).wait()
         for r in range(n * EACH, n * EACH + EACH):
             half[r] = part[r, core] + swap[r]
         for r in range(n * EACH, n * EACH + EACH):
-            if OFFSETS[r]:
-                pltpu.make_async_remote_copy(
-                    src_ref=half.at[r], dst_ref=recv.at[r], send_sem=send_sems.at[0],
-                    recv_sem=recv_sems.at[0], device_id=(chip(OFFSETS[r]), core), device_id_type=MESH).start()
+            give(half.at[r], r, (chip(OFFSETS[r]), core))
 
     def done(n):
         with jax.named_scope("send"):
@@ -395,20 +412,26 @@
                 part[r] = (acc[at, 0:128] + acc[at, 128:256]).reshape(2, 8, 128)
             if n == 0:
                 pl.semaphore_wait(barrier, len(peers))
-            swap_of(n).start()
+            if n < PARTS - 1:
+                swap_of(n).start()
+            else:
+                for r in range(CLOSE, CHIPS):
+                    to = chip(OFFSETS[r])
+                    if r < CHIPS - 1:
+                        give(part.at[r, core], r, (to, core))
+                    give(part.at[r, 1 - core], CHIPS - 1 + r - CLOSE, (to, 1 - core))
 
     with jax.named_scope("points"):
         point_sums(pid_ref, xs, tot, heads, tails, fix, cameras_in)
     with jax.named_scope("cameras"):
         camera_sums(pid_ref, pos_ref, xs, tot, fix, red, ts, rhs, acc, done, send)
     with jax.named_scope("scatter"):
-        send(PARTS - 1)
         pltpu.make_async_copy(recv, recv, recv_sems.at[0]).wait()
 
     with jax.named_scope("invert"):
-        sums = [recv[n] for n in range(CHIPS - 1)] + [half[CHIPS - 1]]
+        sums = [recv[n] for n in range(CHIPS - 1 + EACH)] + [part[CHIPS - 1, core]]
         while len(sums) > 1:
-            sums = [sums[i] + sums[i + 1] for i in range(0, len(sums), 2)]
+            sums = [sums[i] + sums[i + 1] for i in range(0, len(sums) - 1, 2)] + sums[len(sums) & ~1 :]
         owned[...] = invert(sums[0], ent, rows_ref)
         mine[CHIPS - 1] = owned[...]
 
@@ -417,7 +440,8 @@
             pltpu.make_async_remote_copy(
                 src_ref=owned, dst_ref=mine.at[RANK[back(off)]], send_sem=send_sems.at[1],
                 recv_sem=recv_sems.at[1], device_id=(chip(off), core), device_id_type=MESH).start()
-        pltpu.make_async_copy(recv, recv, recv_sems.at[1]).wait()
+        others = recv.at[0 : CHIPS - 1]
+        pltpu.make_async_copy(others, others, recv_sems.at[1]).wait()
     with jax.named_scope("near"):
         across = pltpu.make_async_remote_copy(
             src_ref=mine, dst_ref=theirs, send_sem=swap_sems.at[0], recv_sem=swap_sems.at[PARTS],
@@ -432,7 +456,7 @@
             choose(left, pick_ref, g, 0, store)
     with jax.named_scope("across"):
         pltpu.make_async_copy(recv, recv, send_sems.at[0]).wait()
-        pltpu.make_async_copy(recv, recv, send_sems.at[1]).wait()
+        pltpu.make_async_copy(others, others, send_sems.at[1]).wait()
         across.wait()
 
 
@@ -473,9 +497,9 @@
             vm((1024, 256), F32),
             vm((64, 128), F32),
             vm((CHIPS, 2, 8, 128), F32),
-            vm((CHIPS, 8, 128), F32),
-            vm((CHIPS, 8, 128), F32),
-            vm((CHIPS - 1, 8, 128), F32),
+            vm((CLOSE, 8, 128), F32),
+            vm((CLOSE, 8, 128), F32),
+            vm((CHIPS - 1 + EACH, 8, 128), F32),
             vm((8, 128), F32),
             vm((CHIPS, 8, 128), F32),
             vm((384, 256), BF16),

time: 32.6 us -> 32.5 us (level)
  no operation moved by 1% of the time
where the time goes in v4:
time: 32.5 us; the launch traced here: 32.4 us
  Pallas kernels  31.7 us (98%)
  between operations  0.64 us (2%)
    pallas_call x1, Pallas kernels, shards(): pl.pallas_call(kernel, out_shape=(shape((CHIPS, 8, 128), F32), shape((64,...  28.6 us
    pallas_call x1, Pallas kernels, shards(): pl.pallas_call(last, out_shape=(shape((16, 81), F32), shape((9, 8192), F3...  3.07 us

profile of v4, /device:TPU:1, one launch (start us, length us, event | category | flops | bytes accessed | tf_op | source)
XLA Modules:
  0.0 32.4 jit_solution(15662138244268285602)
XLA Ops:
  0.6 28.6 %schur.1 = (f32[64,8,128]{2,1,0:T(8,128)S(1)}, s32[64,128]{1,0:T(8,128)S(1)}, f32[9,64,128]{2,1,0:T(8,128)S(1)}, f32[128,128]{1,0:T(8,128)S(1)}, f32[3072,128]{1,0:T(8,128)S(1)}) custom-call(f32[18,8192]{1,0:T(8,128)} %cam_hbm.1, f32[6,8192]{1,0:T(8,128)} %pt_hbm.1, f32[2,8192]{1,0:T(2,128)} %res_hbm.1, s32[64,128]{1,0:T(8,128)} %bitcast.4, ...), custom_call_target="tpu_custom_call" | custom-call | tf_op jit(solution)/shard_map/schur/pallas_call | solution.py:470
  29.3 3.1 %last.1 = (f32[16,81]{1,0:T(8,128)}, f32[9,8192]{1,0:T(8,128)}) custom-call(f32[64,8,128]{2,1,0:T(8,128)S(1)} %get-tuple-element.9.theirs, s32[64,128]{1,0:T(8,128)S(1)} %get-tuple-element.10.pick_ref, f32[9,64,128]{2,1,0:T(8,128)S(1)} %get-tuple-element.11.red_ref, f32[128,128]{1,0:T(8,128)S(1)} %get-tuple-element.12.rows_ref, ...), custom_call_target="tpu_custom_call" | custom-call | tf_op jit(solution)/shard_map/last/pallas_call | solution.py:529

commit v5 on v4

--- a/solution.py
+++ b/solution.py
@@ -106,15 +106,11 @@
         heads[pl.ds(m8(g * 8), 8), :] = head
         tails[pl.ds(m8(g * 8), 8), :] = tail
 
-    def step(n, carry):
-        states = [one(n * 4 + u) for u in range(4)]
-        for b in range(7):
-            states = [scan(state, 1 << b) for state in states]
-        for u in range(4):
-            finish(n * 4 + u, states[u])
-        return carry
-
-    lax.fori_loop(0, 2, step, 0)
+    states = [one(g) for g in range(8)]
+    for b in range(7):
+        states = [scan(state, 1 << b) for state in states]
+    for g in range(8):
+        finish(g, states[g])
     between()
 
     pid = pid_ref[...]

time: 32.5 us -> 31.9 us (0.982)
  Pallas kernels: 31.7 us -> 31.1 us
    pallas_call x1, Pallas kernels: 28.6 us -> 28.1 us  [shards(): pl.pallas_call(kernel, out_shape=(shape((CHIPS, 8, 128), F32), shape((64,...]
where the time goes in v5:
time: 31.9 us; the launch traced here: 31.8 us
  Pallas kernels  31.1 us (97%)
  between operations  0.64 us (2%)
    pallas_call x1, Pallas kernels, shards(): pl.pallas_call(kernel, out_shape=(shape((CHIPS, 8, 128), F32), shape((64,...  28.1 us
    pallas_call x1, Pallas kernels, shards(): pl.pallas_call(last, out_shape=(shape((16, 81), F32), shape((9, 8192), F3...  3.07 us

profile of v5, /device:TPU:1, one launch (start us, length us, event | category | flops | bytes accessed | tf_op | source)
XLA Modules:
  0.0 31.8 jit_solution(10746001865163996318)
XLA Ops:
  0.6 28.1 %schur.1 = (f32[64,8,128]{2,1,0:T(8,128)S(1)}, s32[64,128]{1,0:T(8,128)S(1)}, f32[9,64,128]{2,1,0:T(8,128)S(1)}, f32[128,128]{1,0:T(8,128)S(1)}, f32[3072,128]{1,0:T(8,128)S(1)}) custom-call(f32[18,8192]{1,0:T(8,128)} %cam_hbm.1, f32[6,8192]{1,0:T(8,128)} %pt_hbm.1, f32[2,8192]{1,0:T(2,128)} %res_hbm.1, s32[64,128]{1,0:T(8,128)} %bitcast.4, ...), custom_call_target="tpu_custom_call" | custom-call | tf_op jit(solution)/shard_map/schur/pallas_call | solution.py:466
  28.7 3.1 %last.1 = (f32[16,81]{1,0:T(8,128)}, f32[9,8192]{1,0:T(8,128)}) custom-call(f32[64,8,128]{2,1,0:T(8,128)S(1)} %get-tuple-element.9.theirs, s32[64,128]{1,0:T(8,128)S(1)} %get-tuple-element.10.pick_ref, f32[9,64,128]{2,1,0:T(8,128)S(1)} %get-tuple-element.11.red_ref, f32[128,128]{1,0:T(8,128)S(1)} %get-tuple-element.12.rows_ref, ...), custom_call_target="tpu_custom_call" | custom-call | tf_op jit(solution)/shard_map/last/pallas_call | solution.py:525

commit v6 on v5

--- a/solution.py
+++ b/solution.py
@@ -24,7 +24,7 @@
 RANK = {off: r for r, off in enumerate(OFFSETS)}
 PARTS = 4
 EACH = CHIPS // PARTS
-AHEAD = 5
+AHEAD = 6
 CLOSE = 3 * EACH
 
 
@@ -206,12 +206,13 @@
             acc[at, :] = part if g == 0 else acc[at, :] + part
 
     terms(0)
+    terms(1)
     for g in range(8):
         multiply(0, g)
         if g < AHEAD:
             multiply(1, g)
-        if g < 7:
-            terms(g + 1)
+        if g < 6:
+            terms(g + 2)
     done(0)
     for g in range(AHEAD, 8):
         multiply(1, g)
@@ -364,13 +365,14 @@
     pairs = [(pt_hbm, pt_ref), (res_hbm, res_ref), (pid_hbm, pid_ref), (cid_hbm, cid_ref),
              (map_hbm, map_ref), (rank_hbm, rank_ref), (cam_hbm, cam_ref)]
     loads = [pltpu.make_async_copy(src, dst, load_sems.at[n]) for n, (src, dst) in enumerate(pairs)]
-    for load in loads:
+    for load in loads[0:6]:
         load.start()
     barrier = pltpu.get_barrier_semaphore()
     peers = [partner] + [(chip(off), core) for off in OFFSETS[:-1]]
     peers += [(chip(off), 1 - core) for off in OFFSETS[:-1] if off in OFFSETS[CLOSE:] or back(off) in OFFSETS[CLOSE:]]
     for peer in peers:
         pl.semaphore_signal(barrier, inc=1, device_id=peer, device_id_type=MESH)
+    loads[6].start()
 
     with jax.named_scope("load"):
         for load in loads[0:3]:

time: 31.9 us -> 31.8 us (level)
  no operation moved by 1% of the time
where the time goes in v6:
time: 31.8 us; the launch traced here: 31.7 us
  Pallas kernels  31 us (97%)
  between operations  0.64 us (2%)
    pallas_call x1, Pallas kernels, shards(): pl.pallas_call(kernel, out_shape=(shape((CHIPS, 8, 128), F32), shape((64,...  27.9 us
    pallas_call x1, Pallas kernels, shards(): pl.pallas_call(last, out_shape=(shape((16, 81), F32), shape((9, 8192), F3...  3.08 us

profile of v6, /device:TPU:1, one launch (start us, length us, event | category | flops | bytes accessed | tf_op | source)
XLA Modules:
  0.0 31.7 jit_solution(13544630588974212386)
XLA Ops:
  0.6 27.9 %schur.1 = (f32[64,8,128]{2,1,0:T(8,128)S(1)}, s32[64,128]{1,0:T(8,128)S(1)}, f32[9,64,128]{2,1,0:T(8,128)S(1)}, f32[128,128]{1,0:T(8,128)S(1)}, f32[3072,128]{1,0:T(8,128)S(1)}) custom-call(f32[18,8192]{1,0:T(8,128)} %cam_hbm.1, f32[6,8192]{1,0:T(8,128)} %pt_hbm.1, f32[2,8192]{1,0:T(2,128)} %res_hbm.1, s32[64,128]{1,0:T(8,128)} %bitcast.4, ...), custom_call_target="tpu_custom_call" | custom-call | tf_op jit(solution)/shard_map/schur/pallas_call | solution.py:468
  28.6 3.1 %last.1 = (f32[16,81]{1,0:T(8,128)}, f32[9,8192]{1,0:T(8,128)}) custom-call(f32[64,8,128]{2,1,0:T(8,128)S(1)} %get-tuple-element.9.theirs, s32[64,128]{1,0:T(8,128)S(1)} %get-tuple-element.10.pick_ref, f32[9,64,128]{2,1,0:T(8,128)S(1)} %get-tuple-element.11.red_ref, f32[128,128]{1,0:T(8,128)S(1)} %get-tuple-element.12.rows_ref, ...), custom_call_target="tpu_custom_call" | custom-call | tf_op jit(solution)/shard_map/last/pallas_call | solution.py:527

commit v7 on v6

--- a/solution.py
+++ b/solution.py
@@ -288,7 +288,7 @@
     return tile
 
 
-def arrange(tiles, left):
+def arrange(tiles, table):
     lane = lax.broadcasted_iota(I32, (8, 128), 1)
     for h in range(8):
         x = [tiles[h * 8 + e] for e in range(8)]
@@ -299,7 +299,13 @@
                     low, high = x[e], x[e + k]
                     x[e] = jnp.where(upper, pltpu.roll(high, 16 * k, 1), low)
                     x[e + k] = jnp.where(upper, high, pltpu.roll(low, 128 - 16 * k, 1))
-        values = jnp.concatenate(x[0:6], axis=0)
+        for b in range(6):
+            table[h, 8 * b : 8 * b + 8, :] = x[b]
+
+
+def split(table, left):
+    for h in range(8):
+        values = table[h]
         hi = values.astype(BF16)
         lo = (values - hi.astype(F32)).astype(BF16)
         at = pl.ds(128 * (h % 2), 128)
@@ -323,7 +329,7 @@
 
 
 def last(theirs, pick_ref, red_ref, rows_ref, near_ref, inv_ref, out_ref, left, picked, outs):
-    arrange(theirs, left)
+    split(theirs, left)
     inv_ref[...] = jnp.transpose(rows_ref[...])[0:16, 0:81]
     for g in range(8):
         base = (g % 2) * (8 * PS)
@@ -352,7 +358,7 @@
 def kernel(cam_hbm, pt_hbm, res_hbm, pid_hbm, cid_hbm, map_hbm, rank_hbm, theirs, pick_ref, red, rows_ref, near_ref,
            cam_ref, pt_ref, res_ref, pid_ref, cid_ref, map_ref, rank_ref, pos_ref,
            xs, ts, tot, heads, tails, fix, rhs, acc, ent,
-           part, swap, half, recv, owned, mine, left, load_sems, swap_sems, send_sems, recv_sems):
+           part, swap, half, recv, owned, mine, table, left, load_sems, swap_sems, send_sems, recv_sems):
     pts, core = lax.axis_index("pts"), lax.axis_index("grp")
     partner = (pts, 1 - core)
     chip_z = [(((pts >> 4) + d) & 3) << 4 for d in range(4)]
@@ -442,10 +448,11 @@
         pltpu.make_async_copy(others, others, recv_sems.at[1]).wait()
     with jax.named_scope("near"):
         across = pltpu.make_async_remote_copy(
-            src_ref=mine, dst_ref=theirs, send_sem=swap_sems.at[0], recv_sem=swap_sems.at[PARTS],
+            src_ref=table, dst_ref=theirs, send_sem=swap_sems.at[0], recv_sem=swap_sems.at[PARTS],
             device_id=partner, device_id_type=MESH)
+        arrange(mine, table)
+        split(table, left)
         across.start()
-        arrange(mine, left)
         for g in range(8):
             def store(j, r, value):
                 at = (g * 8 + j) * 48 + r
@@ -468,7 +475,7 @@
     theirs, picks, red, rows, near = pl.pallas_call(
         kernel,
         out_shape=(
-            shape((CHIPS, 8, 128), F32),
+            shape((8, 48, 128), F32),
             shape((64, 128), I32),
             shape((9, 64, 128), F32),
             shape((128, 128), F32),
@@ -500,6 +507,7 @@
             vm((CHIPS - 1 + EACH, 8, 128), F32),
             vm((8, 128), F32),
             vm((CHIPS, 8, 128), F32),
+            vm((8, 48, 128), F32),
             vm((384, 256), BF16),
             dma((7,)),
             dma((2 * PARTS,)),

time: 31.8 us -> 31.7 us (level)
  no operation moved by 1% of the time
where the time goes in v7:
time: 31.7 us; the launch traced here: 31.6 us
  Pallas kernels  30.9 us (97%)
  between operations  0.64 us (2%)
    pallas_call x1, Pallas kernels, shards(): pl.pallas_call(kernel, out_shape=(shape((8, 48, 128), F32), shape((64, 12...  28.1 us
    pallas_call x1, Pallas kernels, shards(): pl.pallas_call(last, out_shape=(shape((16, 81), F32), shape((9, 8192), F3...  2.82 us

profile of v7, /device:TPU:1, one launch (start us, length us, event | category | flops | bytes accessed | tf_op | source)
XLA Modules:
  0.0 31.6 jit_solution(15278758632391613909)
XLA Ops:
  0.6 28.1 %schur.1 = (f32[8,48,128]{2,1,0:T(8,128)S(1)}, s32[64,128]{1,0:T(8,128)S(1)}, f32[9,64,128]{2,1,0:T(8,128)S(1)}, f32[128,128]{1,0:T(8,128)S(1)}, f32[3072,128]{1,0:T(8,128)S(1)}) custom-call(f32[18,8192]{1,0:T(8,128)} %cam_hbm.1, f32[6,8192]{1,0:T(8,128)} %pt_hbm.1, f32[2,8192]{1,0:T(2,128)} %res_hbm.1, s32[64,128]{1,0:T(8,128)} %bitcast.4, ...), custom_call_target="tpu_custom_call" | custom-call | tf_op jit(solution)/shard_map/schur/pallas_call | solution.py:475
  28.8 2.8 %last.1 = (f32[16,81]{1,0:T(8,128)}, f32[9,8192]{1,0:T(8,128)}) custom-call(f32[8,48,128]{2,1,0:T(8,128)S(1)} %get-tuple-element.9.theirs, s32[64,128]{1,0:T(8,128)S(1)} %get-tuple-element.10.pick_ref, f32[9,64,128]{2,1,0:T(8,128)S(1)} %get-tuple-element.11.red_ref, f32[128,128]{1,0:T(8,128)S(1)} %get-tuple-element.12.rows_ref, ...), custom_call_target="tpu_custom_call" | custom-call | tf_op jit(solution)/shard_map/last/pallas_call | solution.py:535
